TPU v7x, 32 devices: a whole 2x2x4 slice. The times are simulated.
32 devices in a mesh: seq: 4 (over x, core), mlp: 4 (over z), head: 2 (over y).
Axes of the slice: x: 2, y: 2, z: 4, core: 2. Of those that a mesh axis runs over, the one named last changes fastest.
Arguments:
- tokens: bfloat16 [4096, 2048], P(('seq', 'mlp', 'head')), may hold values from -6 to 6
- cotangent: bfloat16 [4096, 2048], P(('seq', 'mlp', 'head')), may hold values from -6 to 6
- attention_in: float32 [2048, 6144], P('seq', ('mlp', 'head')), may hold values from -0.15467961 to 0.15467961
- feedforward_in: float32 [2048, 12288], P('seq', ('mlp', 'head')), may hold values from -0.15467961 to 0.15467961
- projection_out: float32 [8192, 2048], P(('mlp', 'head'), 'seq'), may hold values from -0.87 to 0.87
- attention_mean: float32 [2048, 6144], P('seq', ('mlp', 'head')), may hold values from -98.56 to 98.56
- feedforward_mean: float32 [2048, 12288], P('seq', ('mlp', 'head')), may hold values from -24.96 to 24.96
- projection_mean: float32 [8192, 2048], P(('mlp', 'head'), 'seq'), may hold values from -30.08 to 30.08
- attention_power: float32 [2048, 6144], P('seq', ('mlp', 'head')), may hold values from 1.024 to 65.536
- feedforward_power: float32 [2048, 12288], P('seq', ('mlp', 'head')), may hold values from 1.024 to 4.096
- projection_power: float32 [8192, 2048], P(('mlp', 'head'), 'seq'), may hold values from 0.16384 to 5.89824
- gains: float32 [4352], replicated, may hold values from 0.8 to 2
- gain_mean: float32 [4352], replicated, may hold values from -115.2 to 115.2
- gain_power: float32 [4352], replicated, may hold values from 4.096 to 262.144
- document_lengths: int32 [4, 8], P('seq'), may hold values from 1 to 512, 1024 in all within a row
- step_count: int32 [1], replicated, may hold values from 2 to 20
Outputs:
- block_output: bfloat16 [4096, 2048], P(('seq', 'mlp', 'head'))
- input_gradient: float32 [4096, 2048], P(('seq', 'mlp', 'head'))
- attention_master: float32 [2048, 6144], P('seq', ('mlp', 'head'))
- feedforward_master: float32 [2048, 12288], P('seq', ('mlp', 'head'))
- projection_master: float32 [8192, 2048], P(('mlp', 'head'), 'seq')
- mean_attention: float32 [2048, 6144], P('seq', ('mlp', 'head'))
- mean_feedforward: float32 [2048, 12288], P('seq', ('mlp', 'head'))
- mean_projection: float32 [8192, 2048], P(('mlp', 'head'), 'seq')
- power_attention: float32 [2048, 6144], P('seq', ('mlp', 'head'))
- power_feedforward: float32 [2048, 12288], P('seq', ('mlp', 'head'))
- power_projection: float32 [8192, 2048], P(('mlp', 'head'), 'seq')
- attention_copy: bfloat16 [2048, 6144], P('seq', ('mlp', 'head'))
- feedforward_copy: bfloat16 [2048, 12288], P('seq', ('mlp', 'head'))
- projection_copy: bfloat16 [8192, 2048], P(('mlp', 'head'), 'seq')
- gains_next: float32 [4352], replicated
- mean_gains: float32 [4352], replicated
- power_gains: float32 [4352], replicated
- matrix_norms: float32 [2, 8], replicated
Inputs may be any that keep to these rules, and one draw needn't show every extreme that they name: `document_lengths`: row s lists, in order, the lengths of the 8 documents packed into sequence s; each row sums to 1024, and its longest document has exactly 512 tokens.
All inputs are finite; a program needn't handle non-finite values.
Results may differ from a plain program's by a relative error of at most 0.022.
Values may be sent and summed in bfloat16 or wider, within the bound.
A program may use at most 192 MiB of HBM per device.

v0:
```python
import math

import jax
import jax.numpy as jnp
from jax import lax
from jax.sharding import PartitionSpec as P

norm_epsilon = 1e-06
rope_base = 1000000.0
beta_one = 0.9
beta_two = 0.999
adam_epsilon = 1e-08
decay_rate = 0.01
learn_rate = 0.3
masked_score = -1e30
highest_precision = lax.Precision.HIGHEST


def scaled_norm(values, norm_gain):
    return (
        values
        * lax.rsqrt(jnp.mean(values * values, axis=-1, keepdims=True) + norm_epsilon)
        * norm_gain
    )


def rotate(values, cosine_table, sine_table):
    middle = values.shape[-1] // 2
    front_half = values[..., :middle]
    back_half = values[..., middle:]
    return jnp.concatenate(
        [
            front_half * cosine_table - back_half * sine_table,
            back_half * cosine_table + front_half * sine_table,
        ],
        axis=-1,
    )


def rotary_tables(position, head_width):
    middle = head_width // 2
    frequency = jnp.exp(
        -(2.0 * jnp.arange(middle, dtype=jnp.float32) / head_width) * math.log(rope_base)
    )
    angles = position.astype(jnp.float32)[:, None] * frequency[None, :]
    return (jnp.cos(angles), jnp.sin(angles))


def document_layout(lengths, total_rows):
    end_points = jnp.cumsum(lengths)
    row_index = jnp.arange(total_rows, dtype=jnp.int32)
    passed = (row_index[:, None] >= end_points[None, :]).astype(jnp.int32)
    segment = jnp.sum(passed, axis=1)
    offset = jnp.sum(passed * lengths[None, :], axis=1)
    return (segment, row_index - offset)


def attention_classes(item_count, group_cols, query_cols, head_width):
    column = jnp.arange(item_count, dtype=jnp.int32) % group_cols
    return jnp.where(
        column < query_cols,
        0,
        jnp.where(
            column < query_cols + head_width,
            1,
            jnp.where(column < query_cols + 2 * head_width, 2, 3),
        ),
    ).astype(jnp.int32)


def forward_classes(item_count, group_cols):
    column = jnp.arange(item_count, dtype=jnp.int32) % group_cols
    return 4 + (column >= group_cols // 2).astype(jnp.int32)


def output_classes(item_count, group_rows, query_cols):
    row_index = jnp.arange(item_count, dtype=jnp.int32) % group_rows
    return 6 + (row_index >= query_cols).astype(jnp.int32)


def indicator_matrix(class_index):
    return (class_index[:, None] == jnp.arange(8, dtype=jnp.int32)[None, :]).astype(jnp.float32)


def kind_sums(matrix, kind_table, over_axis):
    return jnp.dot(
        jnp.sum(matrix * matrix, axis=over_axis), kind_table, precision=highest_precision
    )


def adam_terms(
    weight, gradient, first_moment, second_moment, correct_one, correct_two, decay_weight
):
    first_new = beta_one * first_moment + (1.0 - beta_one) * gradient
    second_new = beta_two * second_moment + (1.0 - beta_two) * gradient * gradient
    direction = (
        first_new / correct_one / (jnp.sqrt(second_new / correct_two) + adam_epsilon)
        + decay_weight * weight
    )
    return (first_new, second_new, direction)


def swiglu(gate_up_product):
    middle = gate_up_product.shape[-1] // 2
    return jax.nn.silu(gate_up_product[:, :middle]) * gate_up_product[:, middle:]


def contract_first(left, right):
    return lax.dot_general(
        left, right, (((0,), (0,)), ((), ())), preferred_element_type=jnp.float32
    )


def contract_last(left, right):
    return lax.dot_general(
        left, right, (((1,), (1,)), ((), ())), preferred_element_type=jnp.float32
    )


def visibility(segment, begin_row, end_row):
    row_index = jnp.arange(begin_row, end_row, dtype=jnp.int32)
    key_index = jnp.arange(end_row, dtype=jnp.int32)
    same_document = segment[begin_row:end_row, None] == segment[None, :end_row]
    return same_document & (key_index[None, :] <= row_index[:, None])


def block_scores(query_low, key_low, visible, begin_row, end_row, scaling):
    scores = (
        jnp.einsum(
            "qhd,kd->hqk",
            query_low[begin_row:end_row],
            key_low[:end_row],
            preferred_element_type=jnp.float32,
        )
        * scaling
    )
    return jnp.where(visible[None], scores, masked_score)


def shards(
    tokens,
    cotangent,
    attention_in,
    feedforward_in,
    projection_out,
    attention_mean,
    feedforward_mean,
    projection_mean,
    attention_power,
    feedforward_power,
    projection_power,
    gains,
    gain_mean,
    gain_power,
    document_lengths,
    step_count,
):
    own_rows = tokens.shape[0]
    model_width = tokens.shape[1]
    total_rows = own_rows * lax.axis_size(("mlp", "head"))
    head_width = (gains.shape[0] - 2 * model_width) // 2
    attention_cols = attention_in.shape[1]
    query_cols = attention_cols // 2 - head_width
    query_heads = query_cols // head_width
    feed_cols = feedforward_in.shape[1]
    output_rows = projection_out.shape[0]
    gain_one = gains[:model_width]
    gain_two = gains[model_width : 2 * model_width]
    gain_query = gains[2 * model_width : 2 * model_width + head_width]
    gain_key = gains[2 * model_width + head_width :]
    attention_lookup = indicator_matrix(
        attention_classes(attention_cols, attention_cols, query_cols, head_width)
    )
    forward_lookup = indicator_matrix(forward_classes(feed_cols, feed_cols))
    output_lookup = indicator_matrix(output_classes(output_rows, output_rows, query_cols))
    weight_local = (
        kind_sums(attention_in, attention_lookup, 0)
        + kind_sums(feedforward_in, forward_lookup, 0)
        + kind_sums(projection_out, output_lookup, 1)
    )
    attention_reduced, forward_reduced, output_reduced = (
        lax.all_gather(attention_in.astype(jnp.bfloat16), "seq", axis=0, tiled=True),
        lax.all_gather(feedforward_in.astype(jnp.bfloat16), "seq", axis=0, tiled=True),
        lax.all_gather(projection_out.astype(jnp.bfloat16), "seq", axis=1, tiled=True),
    )
    mixer_low = output_reduced[:query_cols]
    down_low = output_reduced[query_cols:]
    segment, position = document_layout(document_lengths[0], total_rows)
    cosine_table, sine_table = rotary_tables(position, head_width)
    inputs = tokens.astype(jnp.float32)
    normed_input, back_one = jax.vjp(scaled_norm, inputs, gain_one)
    normed_rows = lax.all_gather(
        normed_input.astype(jnp.bfloat16), ("mlp", "head"), axis=0, tiled=True
    )
    projected_rows = jnp.dot(normed_rows, attention_reduced, preferred_element_type=jnp.float32)
    query_rows = projected_rows[:, :query_cols].reshape(total_rows, query_heads, head_width)
    keys_raw = projected_rows[:, query_cols : query_cols + head_width]
    values_low = projected_rows[:, query_cols + head_width : query_cols + 2 * head_width].astype(
        jnp.bfloat16
    )
    gate_scores_raw = projected_rows[:, query_cols + 2 * head_width :]

    def prepare(query_in, key_in, query_gain, key_gain):
        query_out = rotate(
            scaled_norm(query_in, query_gain), cosine_table[:, None, :], sine_table[:, None, :]
        )
        key_out = rotate(scaled_norm(key_in, key_gain), cosine_table, sine_table)
        return (query_out, key_out)

    (query_rot, key_rot), back_prepare = jax.vjp(
        prepare, query_rows, keys_raw, gain_query, gain_key
    )
    query_low = query_rot.astype(jnp.bfloat16)
    key_low = key_rot.astype(jnp.bfloat16)
    block_rows = min(512, total_rows)
    block_count = total_rows // block_rows
    scaling = head_width ** (-0.5)
    pieces = []
    log_totals = []
    for block_index in range(block_count):
        begin_row = block_index * block_rows
        end_row = begin_row + block_rows
        visible = visibility(segment, begin_row, end_row)
        scores = block_scores(query_low, key_low, visible, begin_row, end_row, scaling)
        row_max = jnp.max(scores, axis=-1, keepdims=True)
        log_total = row_max + jnp.log(jnp.sum(jnp.exp(scores - row_max), axis=-1, keepdims=True))
        softmax_low = jnp.exp(scores - log_total).astype(jnp.bfloat16)
        pieces.append(
            jnp.einsum(
                "hqk,kd->qhd", softmax_low, values_low[:end_row], preferred_element_type=jnp.float32
            )
        )
        log_totals.append(log_total)
    attended_rows = jnp.concatenate(pieces, axis=0).reshape(total_rows, query_cols)
    gate_sigmoid = jax.nn.sigmoid(gate_scores_raw)
    gated_low = (attended_rows * gate_sigmoid).astype(jnp.bfloat16)
    attention_out = lax.psum_scatter(
        jnp.dot(gated_low, mixer_low, preferred_element_type=jnp.float32),
        ("mlp", "head"),
        scatter_dimension=0,
        tiled=True,
    )
    middle = inputs + attention_out
    normed_second, back_two = jax.vjp(scaled_norm, middle, gain_two)
    feed_rows = lax.all_gather(
        normed_second.astype(jnp.bfloat16), ("mlp", "head"), axis=0, tiled=True
    )
    gate_up_product = jnp.dot(feed_rows, forward_reduced, preferred_element_type=jnp.float32)
    activated, back_swiglu = jax.vjp(swiglu, gate_up_product)
    activated_low = activated.astype(jnp.bfloat16)
    feed_out = lax.psum_scatter(
        jnp.dot(activated_low, down_low, preferred_element_type=jnp.float32).astype(jnp.bfloat16),
        ("mlp", "head"),
        scatter_dimension=0,
        tiled=True,
    ).astype(jnp.float32)
    block_output = (middle + feed_out).astype(jnp.bfloat16)
    cotangent_rows = lax.all_gather(cotangent, ("mlp", "head"), axis=0, tiled=True)
    delta_activated = contract_last(cotangent_rows, down_low)
    delta_gate_up = back_swiglu(delta_activated)[0].astype(jnp.bfloat16)
    down_gradient = contract_first(activated_low, cotangent_rows)
    feed_gradient = contract_first(feed_rows, delta_gate_up)
    delta_normed_two = lax.psum_scatter(
        contract_last(delta_gate_up, forward_reduced),
        ("mlp", "head"),
        scatter_dimension=0,
        tiled=True,
    )
    delta_middle_part, delta_gain_two = back_two(delta_normed_two)
    delta_middle = cotangent.astype(jnp.float32) + delta_middle_part
    branch_rows = lax.all_gather(
        delta_middle.astype(jnp.bfloat16), ("mlp", "head"), axis=0, tiled=True
    )
    delta_gated = contract_last(branch_rows, mixer_low)
    mixer_gradient = contract_first(gated_low, branch_rows)
    delta_attended = delta_gated * gate_sigmoid
    delta_logits = delta_gated * attended_rows * gate_sigmoid * (1.0 - gate_sigmoid)
    delta_attended_low = delta_attended.astype(jnp.bfloat16).reshape(
        total_rows, query_heads, head_width
    )
    query_deltas = []
    key_delta = jnp.zeros((total_rows, head_width), jnp.float32)
    value_delta = jnp.zeros((total_rows, head_width), jnp.float32)
    for block_index in range(block_count):
        begin_row = block_index * block_rows
        end_row = begin_row + block_rows
        visible = visibility(segment, begin_row, end_row)
        scores = block_scores(query_low, key_low, visible, begin_row, end_row, scaling)
        softmax_full = jnp.exp(scores - log_totals[block_index])
        softmax_low = softmax_full.astype(jnp.bfloat16)
        delta_rows = delta_attended_low[begin_row:end_row]
        delta_softmax = jnp.einsum(
            "qhd,kd->hqk", delta_rows, values_low[:end_row], preferred_element_type=jnp.float32
        )
        inner_sum = jnp.sum(softmax_full * delta_softmax, axis=-1, keepdims=True)
        delta_scores = (softmax_full * (delta_softmax - inner_sum)).astype(jnp.bfloat16)
        query_deltas.append(
            jnp.einsum(
                "hqk,kd->qhd", delta_scores, key_low[:end_row], preferred_element_type=jnp.float32
            )
            * scaling
        )
        key_delta = key_delta.at[:end_row].add(
            jnp.einsum(
                "hqk,qhd->kd",
                delta_scores,
                query_low[begin_row:end_row],
                preferred_element_type=jnp.float32,
            )
            * scaling
        )
        value_delta = value_delta.at[:end_row].add(
            jnp.einsum("hqk,qhd->kd", softmax_low, delta_rows, preferred_element_type=jnp.float32)
        )
    query_delta = jnp.concatenate(query_deltas, axis=0)
    query_back, key_back, delta_gain_query, delta_gain_key = back_prepare((query_delta, key_delta))
    delta_projected = jnp.concatenate(
        [query_back.reshape(total_rows, query_cols), key_back, value_delta, delta_logits], axis=1
    ).astype(jnp.bfloat16)
    delta_normed = lax.psum_scatter(
        contract_last(delta_projected, attention_reduced).astype(jnp.bfloat16),
        ("mlp", "head"),
        scatter_dimension=0,
        tiled=True,
    ).astype(jnp.float32)
    delta_input_part, delta_gain_one = back_one(delta_normed)
    input_gradient = delta_middle + delta_input_part
    attention_gradient = contract_first(normed_rows, delta_projected)
    output_gradient = jnp.concatenate([mixer_gradient, down_gradient], axis=0)
    attention_total, feed_total, output_total = (
        lax.psum_scatter(
            attention_gradient.astype(jnp.bfloat16), "seq", scatter_dimension=0, tiled=True
        ).astype(jnp.float32),
        lax.psum_scatter(
            feed_gradient.astype(jnp.bfloat16), "seq", scatter_dimension=0, tiled=True
        ).astype(jnp.float32),
        lax.psum_scatter(
            output_gradient.astype(jnp.bfloat16), "seq", scatter_dimension=1, tiled=True
        ).astype(jnp.float32),
    )
    steps_done = step_count[0].astype(jnp.float32)
    correct_one = 1.0 - jnp.power(beta_one, steps_done)
    correct_two = 1.0 - jnp.power(beta_two, steps_done)
    mean_attention, power_attention, move_attention = adam_terms(
        attention_in,
        attention_total,
        attention_mean,
        attention_power,
        correct_one,
        correct_two,
        decay_rate,
    )
    mean_feedforward, power_feedforward, move_feed = adam_terms(
        feedforward_in,
        feed_total,
        feedforward_mean,
        feedforward_power,
        correct_one,
        correct_two,
        decay_rate,
    )
    mean_projection, power_projection, move_output = adam_terms(
        projection_out,
        output_total,
        projection_mean,
        projection_power,
        correct_one,
        correct_two,
        decay_rate,
    )
    update_local = (
        kind_sums(move_attention, attention_lookup, 0)
        + kind_sums(move_feed, forward_lookup, 0)
        + kind_sums(move_output, output_lookup, 1)
    )
    gain_local = jnp.concatenate([delta_gain_one, delta_gain_two, delta_gain_query, delta_gain_key])
    norm_local = jnp.concatenate([weight_local, update_local])
    gain_total, norm_total = lax.psum((gain_local, norm_local), ("seq", "mlp", "head"))
    weight_squares = norm_total[:8]
    update_squares = norm_total[8:]
    trust_ratio = jnp.sqrt(weight_squares) / jnp.sqrt(update_squares)
    attention_master = (
        attention_in
        - learn_rate
        * jnp.dot(attention_lookup, trust_ratio, precision=highest_precision)[None, :]
        * move_attention
    )
    feedforward_master = (
        feedforward_in
        - learn_rate
        * jnp.dot(forward_lookup, trust_ratio, precision=highest_precision)[None, :]
        * move_feed
    )
    projection_master = (
        projection_out
        - learn_rate
        * jnp.dot(output_lookup, trust_ratio, precision=highest_precision)[:, None]
        * move_output
    )
    mean_gains, power_gains, move_gains = adam_terms(
        gains, gain_total, gain_mean, gain_power, correct_one, correct_two, 0.0
    )
    gains_next = gains - learn_rate * move_gains
    matrix_norms = jnp.stack([jnp.sqrt(weight_squares), jnp.sqrt(update_squares)])
    return (
        block_output,
        input_gradient,
        attention_master,
        feedforward_master,
        projection_master,
        mean_attention,
        mean_feedforward,
        mean_projection,
        power_attention,
        power_feedforward,
        power_projection,
        attention_master.astype(jnp.bfloat16),
        feedforward_master.astype(jnp.bfloat16),
        projection_master.astype(jnp.bfloat16),
        gains_next,
        mean_gains,
        power_gains,
        matrix_norms,
    )


def solution(mesh):
    placed = (
        P(("seq", "mlp", "head"), None),
        P(("seq", "mlp", "head"), None),
        P("seq", ("mlp", "head")),
        P("seq", ("mlp", "head")),
        P(("mlp", "head"), "seq"),
        P("seq", ("mlp", "head")),
        P("seq", ("mlp", "head")),
        P(("mlp", "head"), "seq"),
        P("seq", ("mlp", "head")),
        P("seq", ("mlp", "head")),
        P(("mlp", "head"), "seq"),
        P(),
        P(),
        P(),
        P("seq", None),
        P(),
    )
    return jax.shard_map(
        shards,
        mesh=mesh,
        in_specs=placed,
        out_specs=(
            P(("seq", "mlp", "head"), None),
            P(("seq", "mlp", "head"), None),
            P("seq", ("mlp", "head")),
            P("seq", ("mlp", "head")),
            P(("mlp", "head"), "seq"),
            P("seq", ("mlp", "head")),
            P("seq", ("mlp", "head")),
            P(("mlp", "head"), "seq"),
            P("seq", ("mlp", "head")),
            P("seq", ("mlp", "head")),
            P(("mlp", "head"), "seq"),
            P("seq", ("mlp", "head")),
            P("seq", ("mlp", "head")),
            P(("mlp", "head"), "seq"),
            P(),
            P(),
            P(),
            P(),
        ),
        check_vma=False,
    )
```

profile of v0, /device:TPU:0, one launch (start us, length us, event | category | flops | bytes accessed | tf_op | source)
XLA Modules:
  0.0 1091.5 jit_solution(9520035271148950967)
XLA Ops:
  7.3 3.6 multiply_reduce_fusion.5
  12.9 1.8 multiply_reduce_fusion.3
  16.6 25.7 %all-gather.10.cloned.1.call-done = bf16[2048,768]{1,0:T(8,128)(2,1)} async-done(((bf16[512,768]{1,0:T(8,128)(2,1)}), bf16[2048,768]{1,0:T(8,128)(2,1)}) %all-gather.10.cloned.1.call-update) | async-done | bytes 3145744 | tf_op jit(solution)/shard_map/all_gather | solution.py:182
  42.3 75.5 %all-gather.8.cloned.1.call-done = bf16[1024,2048]{1,0:T(8,128)(2,1)} async-done(((bf16[128,2048]{1,0:T(8,128)(2,1)}), bf16[1024,2048]{1,0:T(8,128)(2,1)}) %all-gather.8.cloned.1.call-update) | async-done | bytes 4194320 | tf_op jit(solution)/shard_map/all_gather | solution.py:192
  117.9 7.9 fusion.139
  125.8 1.2 slice.191
  128.0 1.4 fusion.73
  129.9 1.7 copy.58
  131.6 1.7 multiply_reduce_fusion.11
  137.8 1.5 convolution_bitcast_fusion.3
  139.3 2.3 convolution_bitcast_fusion.2
  142.7 1.6 fusion.45
  144.3 8.7 all-gather.12.cloned.1.call-done
  153.0 5.8 fusion.52
  158.9 5.0 multiply_reduce_fusion.1
  164.0 142.4 %reduce-scatter.8.cloned.1.call-done = f32[128,2048]{1,0:T(8,128)} async-done(((f32[1024,2048]{1,0:T(8,128)}), f32[128,2048]{1,0:T(8,128)}) %reduce-scatter.8.cloned.1.call-update) | async-done | bytes 1048592 | tf_op jit(solution)/shard_map/reduce_scatter | solution.py:237
  306.4 1.6 multiply_reduce_fusion.10
  308.1 1.1 multiply_convert_fusion.2
  310.0 44.0 %all-gather.16.cloned.1.call-done = bf16[2048,1536]{1,0:T(8,128)(2,1)} async-done(((bf16[512,1536]{1,0:T(8,128)(2,1)}), bf16[2048,1536]{1,0:T(8,128)(2,1)}) %all-gather.16.cloned.1.call-update) | async-done | bytes 6291472 | tf_op jit(solution)/shard_map/all_gather | solution.py:183
  353.9 75.4 %all-gather.14.cloned.1.call-done = bf16[1024,2048]{1,0:T(8,128)(2,1)} async-done(((bf16[128,2048]{1,0:T(8,128)(2,1)}), bf16[1024,2048]{1,0:T(8,128)(2,1)}) %all-gather.14.cloned.1.call-update) | async-done | bytes 4194320 | tf_op jit(solution)/shard_map/all_gather | solution.py:245
  429.3 12.1 %fusion.141 = f32[1024,1536]{1,0:T(8,128)} fusion(bf16[1024,2048]{1,0:T(8,128)(2,1)} %all-gather.14.cloned.1.call-done, bf16[2048,1536]{1,0:T(8,128)(2,1)} %all-gather.16.cloned.1.call-done), kind=kOutput, calls=%fused_computation.265 | convolution fusion | flops 6442450944 | bytes 16777216 | tf_op jit(solution)/shard_map/dot_general | solution.py:248
  441.5 61.3 %all-gather.18.cloned.1.call-done = bf16[1024,2048]{1,0:T(8,128)(2,1)} async-done(((bf16[128,2048]{1,0:T(8,128)(2,1)}), bf16[1024,2048]{1,0:T(8,128)(2,1)}) %all-gather.18.cloned.1.call-update) | async-done | bytes 4194320 | tf_op jit(solution)/shard_map/all_gather | solution.py:258
  502.8 10.6 fusion.68
  513.4 1.7 copy-done.79
  515.0 1.0 copy-done.80
  516.1 9.0 fusion.56
  525.2 146.1 %reduce-scatter.12.cloned.1.call-done = f32[128,2048]{1,0:T(8,128)} async-done(((f32[1024,2048]{1,0:T(8,128)}), f32[128,2048]{1,0:T(8,128)}) %reduce-scatter.12.cloned.1.call-update) | async-done | bytes 1048592 | tf_op jit(solution)/shard_map/reduce_scatter | solution.py:263
  671.3 2.1 multiply_reduce_fusion.7
  673.4 2.5 fusion.124
  676.0 12.3 %convolution_convert_fusion = bf16[2048,1536]{1,0:T(8,128)(2,1)} fusion(bf16[1024,2048]{1,0:T(8,128)(2,1)} %all-gather.14.cloned.1.call-done, f32[1024,768]{1,0:T(8,128)} %copy-done.80, f32[1024,768]{1,0:T(8,128)} %copy-done.79), kind=kOutput, calls=%fused_computation | convolution fusion | flops 6448742400 | bytes 16777216 | tf_op jit(solution)/shard_map/dot_general | solution.py:109
  688.4 59.6 %all-gather.20.cloned.1.call-done = bf16[1024,2048]{1,0:T(8,128)(2,1)} async-done(((bf16[128,2048]{1,0:T(8,128)(2,1)}), bf16[1024,2048]{1,0:T(8,128)(2,1)}) %all-gather.20.cloned.1.call-update) | async-done | bytes 4194320 | tf_op jit(solution)/shard_map/all_gather | solution.py:271
  747.9 5.0 multiply_convert_fusion.1
  753.0 1.5 fusion.15
  757.0 2.5 fusion
  759.5 1.3 fusion.2
  764.5 1.9 fusion.38
  766.4 2.1 copy.75
  768.4 1.7 fusion.30
  770.2 1.9 fusion.26
  772.2 1.2 fusion.76
  773.4 1.4 multiply_reduce_fusion.12
  775.3 1.2 fusion.54
  776.6 1.4 fusion.29
  779.0 4.9 convolution_convert_fusion.4
  784.0 6.9 convolution_convert_fusion.1
  791.0 1.3 copy-done.77
  792.4 6.0 convolution_convert_fusion.3
  798.4 1.3 convolution_convert_fusion.5
  799.7 2.4 pad_maximum_fusion
  802.1 7.1 convolution_convert_fusion.2
  811.5 6.7 multiply_reduce_fusion
  818.3 30.5 %reduce-scatter.16.cloned.1.call-done = bf16[512,768]{1,0:T(8,128)(2,1)} async-done(((bf16[2048,768]{1,0:T(8,128)(2,1)}), bf16[512,768]{1,0:T(8,128)(2,1)}) %reduce-scatter.16.cloned.1.call-update) | async-done | bytes 786448 | tf_op jit(solution)/shard_map/reduce_scatter | solution.py:331
  848.8 5.5 multiply_reduce_fusion.4
  854.6 85.9 %reduce-scatter.14.cloned.1.call-done = bf16[128,2048]{1,0:T(8,128)(2,1)} async-done(((bf16[1024,2048]{1,0:T(8,128)(2,1)}), bf16[128,2048]{1,0:T(8,128)(2,1)}) %reduce-scatter.14.cloned.1.call-update) | async-done | bytes 524304 | tf_op jit(solution)/shard_map/reduce_scatter | solution.py:320
  940.6 1.8 fusion.36
  942.4 44.8 %reduce-scatter.20.cloned.1.call-done = bf16[1024,512]{1,0:T(8,128)(2,1)} async-done(((bf16[1024,2048]{1,0:T(8,128)(2,1)}), bf16[1024,512]{1,0:T(8,128)(2,1)}) %reduce-scatter.20.cloned.1.call-update) | async-done | bytes 1048592 | tf_op jit(solution)/shard_map/reduce_scatter | solution.py:337
  987.2 7.5 multiply_reduce_fusion.2
  995.6 42.3 %all-reduce.8 = (f32[16]{0:T(128)S(1)}, f32[4352]{0:T(1024)S(1)}) all-reduce(f32[16]{0:T(128)S(1)} %pad_maximum_fusion.10, f32[4352]{0:T(1024)S(1)} %pad_maximum_fusion.8), channel_id=1, replica_groups=mesh['seq'=4,'mlp'=4,'head'=2] {'seq','mlp','head'}, use_global_device_ids=true, to_apply=%region_30.31 | all-reduce | flops 4368 | bytes 34944 | tf_op jit(solution)/shard_map/psum | solution.py:378
  1040.7 3.5 fusion.128
  1044.3 2.0 fusion.126
  1046.2 1.1 copy-done.12
  1047.3 3.0 fusion.127
  1050.3 30.4 %reduce-scatter.10.cloned.1.call-done = bf16[128,2048]{1,0:T(8,128)(2,1)} async-done(((bf16[1024,2048]{1,0:T(8,128)(2,1)}), bf16[128,2048]{1,0:T(8,128)(2,1)}) %reduce-scatter.10.cloned.1.call-update) | async-done | bytes 524304 | tf_op jit(solution)/shard_map/reduce_scatter | solution.py:251
  1080.7 3.8 fusion.39
  (252 shorter events, 24.7 us)
Async XLA Ops:
  7.2 3.8 copy-start.11
  7.2 4.6 copy-start.42
  7.2 5.7 copy-start.5
  7.2 35.1 %all-gather.10.cloned.1.call-start = ((), (), s32[]{:S(2)}) async-start(), calls=%async_computation.8 | async-start | bytes 3932160 | tf_op jit(solution)/shard_map/all_gather | solution.py:182
  10.9 3.9 copy-start.73
  11.0 106.9 %all-gather.8.cloned.1.call-start = ((), (), s32[]{:S(2)}) async-start(), calls=%async_computation.7 | async-start | bytes 4718592 | tf_op jit(solution)/shard_map/all_gather | solution.py:192
  11.8 3.4 copy-start.64
  11.8 4.8 copy-start.35
  12.8 140.2 %all-gather.12.cloned.1.call-start = ((), (), s32[]{:S(2)}) async-start(), calls=%async_computation.9 | async-start | bytes 5242880 | tf_op jit(solution)/shard_map/all_gather | solution.py:184
  14.7 291.7 %reduce-scatter.8.cloned.1.call-start = ((), (), s32[]{:S(2)}) async-start(), calls=%async_computation.10 | async-start | bytes 9437184 | tf_op jit(solution)/shard_map/reduce_scatter | solution.py:237
  14.8 113.2 %copy-start.67 = (f32[64]{0:T(128)}, f32[64]{0:T(128)S(1)}, u32[]{:S(2)}) copy-start(f32[64]{0:T(128)S(1)} %multiply_exponential_fusion) | copy-start | bytes 772
  15.1 112.9 %copy-start.49 = (f32[1024]{0:T(1024)}, f32[1024]{0:T(1024)S(1)}, u32[]{:S(2)}) copy-start(f32[1024]{0:T(1024)S(1)} %subtract_convert_fusion.1) | copy-start | bytes 12292
  15.2 111.9 %copy-start.58 = (f32[128]{0:T(128)}, f32[128]{0:T(128)S(1)}, u32[]{:S(2)}) copy-start(f32[128]{0:T(128)S(1)} %get-tuple-element.142) | copy-start | bytes 1540
  15.2 118.2 %copy-start.60 = (f32[128]{0:T(128)}, f32[128]{0:T(128)S(1)}, u32[]{:S(2)}) copy-start(f32[128]{0:T(128)S(1)} %get-tuple-element.143) | copy-start | bytes 1540
  16.6 122.8 %copy-start.15 = (pred[512,1024]{0,1:T(8,128)(4,1)}, pred[512,1024]{0,1:T(8,128)(4,1)S(1)}, u32[]{:S(2)}) copy-start(pred[512,1024]{0,1:T(8,128)(4,1)S(1)} %fusion.18) | copy-start | bytes 1572868
  127.0 6.3 copy-start.51
  129.4 6.2 copy-start.28
  129.6 4.6 copy-start.20
  129.9 4.4 copy-start.22
  131.6 2.6 copy-start.9
  137.8 3.9 copy-start.46
  144.3 14.5 %copy-start.26 = (bf16[1024,256]{0,1:T(8,128)(2,1)}, bf16[1024,256]{0,1:T(8,128)(2,1)S(1)}, u32[]{:S(2)}) copy-start(bf16[1024,256]{0,1:T(8,128)(2,1)S(1)} %fusion.45) | copy-start | bytes 1572868
  158.8 195.1 %all-gather.16.cloned.1.call-start = ((), (), s32[]{:S(2)}) async-start(), calls=%async_computation.12 | async-start | bytes 7864320 | tf_op jit(solution)/shard_map/all_gather | solution.py:183
  164.0 265.4 %all-gather.14.cloned.1.call-start = ((), (), s32[]{:S(2)}) async-start(), calls=%async_computation.11 | async-start | bytes 4718592 | tf_op jit(solution)/shard_map/all_gather | solution.py:245
  308.0 365.3 %copy-start.4 = (f32[128,2048]{1,0:T(8,128)}, f32[128,2048]{1,0:T(8,128)S(1)}, u32[]{:S(2)}) copy-start(f32[128,2048]{1,0:T(8,128)S(1)} %get-tuple-element.116) | copy-start | bytes 3145732
  308.0 365.3 %copy-start.62 = (f32[128]{0:T(128)}, f32[128]{0:T(128)S(1)}, u32[]{:S(2)}) copy-start(f32[128]{0:T(128)S(1)} %fusion.105) | copy-start | bytes 1540
  309.2 193.6 %all-gather.18.cloned.1.call-start = ((), (), s32[]{:S(2)}) async-start(), calls=%async_computation.14 | async-start | bytes 4718592 | tf_op jit(solution)/shard_map/all_gather | solution.py:258
  309.9 361.4 %reduce-scatter.12.cloned.1.call-start = ((), (), s32[]{:S(2)}) async-start(), calls=%async_computation.15 | async-start | bytes 9437184 | tf_op jit(solution)/shard_map/reduce_scatter | solution.py:263
  502.8 13.3 %copy-start.74 = (bf16[2048,1536]{1,0:T(8,128)(2,1)S(1)}, bf16[2048,1536]{1,0:T(8,128)(2,1)}, u32[]{:S(2)}) copy-start(bf16[2048,1536]{1,0:T(8,128)(2,1)} %all-gather.16.cloned.1.call-done) | copy-start | bytes 18874372
  513.4 2.7 copy-start.80
  525.1 222.8 %all-gather.20.cloned.1.call-start = ((), (), s32[]{:S(2)}) async-start(), calls=%async_computation.16 | async-start | bytes 4718592 | tf_op jit(solution)/shard_map/all_gather | solution.py:271
  673.4 14.9 %copy-start.69 = (f32[128]{0:T(128)}, f32[128]{0:T(128)S(1)}, u32[]{:S(2)}) copy-start(f32[128]{0:T(128)S(1)} %multiply_multiply_fusion.9) | copy-start | bytes 1540
  675.9 135.6 %reduce-scatter.18.cloned.1.call-start = ((), (), s32[]{:S(2)}) async-start(), calls=%async_computation.19 | async-start | bytes 7864320 | tf_op jit(solution)/shard_map/reduce_scatter | solution.py:334
  688.3 59.7 %copy-start.25 = (f32[1024,2,128]{0,2,1:T(8,128)S(1)}, f32[1024,2,128]{0,2,1:T(8,128)}, u32[]{:S(2)}) copy-start(f32[1024,2,128]{0,2,1:T(8,128)} %copy-done.24) | copy-start | bytes 3145732
  688.3 160.5 %reduce-scatter.16.cloned.1.call-start = ((), (), s32[]{:S(2)}) async-start(), calls=%async_computation.18 | async-start | bytes 3932160 | tf_op jit(solution)/shard_map/reduce_scatter | solution.py:331
  753.0 3.0 copy-start.32
  760.8 2.6 copy-start.7
  766.4 5.7 copy-start.50
  766.4 5.7 copy-start.68
  768.4 4.9 copy-start.45
  768.4 4.9 copy-start.59
  770.2 4.6 copy-start.39
  770.2 5.1 copy-start.52
  772.1 4.4 copy-start.2
  772.1 4.4 copy-start.17
  772.1 4.4 copy-start.33
  772.1 4.4 copy-start.48
  784.0 156.6 %reduce-scatter.14.cloned.1.call-start = ((), (), s32[]{:S(2)}) async-start(), calls=%async_computation.17 | async-start | bytes 4718592 | tf_op jit(solution)/shard_map/reduce_scatter | solution.py:320
  791.0 196.2 %reduce-scatter.20.cloned.1.call-start = ((), (), s32[]{:S(2)}) async-start(), calls=%async_computation.20 | async-start | bytes 5242880 | tf_op jit(solution)/shard_map/reduce_scatter | solution.py:337
  792.4 6.0 copy-start.27
  792.4 6.1 copy-start.76
  802.1 278.6 %reduce-scatter.10.cloned.1.call-start = ((), (), s32[]{:S(2)}) async-start(), calls=%async_computation.13 | async-start | bytes 4718592 | tf_op jit(solution)/shard_map/reduce_scatter | solution.py:251
  818.2 122.3 %copy-start.36 = (f32[2048]{0:T(1024)S(1)}, f32[2048]{0:T(1024)}, u32[]{:S(2)}) copy-start(f32[2048]{0:T(1024)} %copy-done.35) | copy-start | bytes 24580
  818.2 122.3 %copy-start.65 = (f32[128]{0:T(128)S(1)}, f32[128]{0:T(128)}, u32[]{:S(2)}) copy-start(f32[128]{0:T(128)} %copy-done.64) | copy-start | bytes 1540
  818.3 124.1 %copy-start.53 = (f32[2048]{0:T(1024)S(1)}, f32[2048]{0:T(1024)}, u32[]{:S(2)}) copy-start(f32[2048]{0:T(1024)} %get-tuple-element.86) | copy-start | bytes 24580
  942.3 97.2 %copy-start.72 = (f32[128]{0:T(128)S(1)}, f32[128]{0:T(128)}, u32[]{:S(2)}) copy-start(f32[128]{0:T(128)} %copy-done.71) | copy-start | bytes 1540
  942.4 97.7 %copy-start.43 = (f32[4352]{0:T(1024)S(1)}, f32[4352]{0:T(1024)}, u32[]{:S(2)}) copy-start(f32[4352]{0:T(1024)} %param.39) | copy-start | bytes 52228
  942.4 97.7 %copy-start.55 = (f32[4352]{0:T(1024)S(1)}, f32[4352]{0:T(1024)}, u32[]{:S(2)}) copy-start(f32[4352]{0:T(1024)} %param.41) | copy-start | bytes 52228
  942.4 97.7 %copy-start.56 = (f32[4352]{0:T(1024)S(1)}, f32[4352]{0:T(1024)}, u32[]{:S(2)}) copy-start(f32[4352]{0:T(1024)} %param.40) | copy-start | bytes 52228
  1037.9 6.4 copy-start.6
  1037.9 6.4 copy-start.14
  1044.3 3.1 copy-start.12
  1047.3 33.4 %copy-start.63 = (f32[128]{0:T(128)S(1)}, f32[128]{0:T(128)}, u32[]{:S(2)}) copy-start(f32[128]{0:T(128)} %copy-done.62) | copy-start | bytes 1540
  1047.3 33.4 %copy-start.70 = (f32[128]{0:T(128)S(1)}, f32[128]{0:T(128)}, u32[]{:S(2)}) copy-start(f32[128]{0:T(128)} %copy-done.69) | copy-start | bytes 1540
  (31 other events, 52.7 us)
Sparse Core Ops, SparseCore 0:
  11.1 31.2 all-gather.9
  45.0 72.7 all-gather.7
  120.0 32.9 all-gather.11
  159.0 147.4 reduce-scatter.7
  308.4 45.4 all-gather.15
  356.5 72.7 all-gather.13
  431.4 71.3 all-gather.17
  525.2 146.0 reduce-scatter.11
  676.0 71.8 all-gather.19
  750.3 57.3 reduce-scatter.17
  810.8 37.9 reduce-scatter.15
  852.2 88.2 reduce-scatter.13
  943.1 44.0 reduce-scatter.19
  990.6 90.0 reduce-scatter.9
where the time goes:
time: 1100 us; the launch traced here: 1090 us
  waiting for transfers between devices  831 us (76%)
  matrix products  109 us (10%)
  other arithmetic  74.4 us (7%)
  blocking collectives  42.3 us (4%)
  local copies, waits for them, and re-layouts  17 us (2%)
  between operations  16.6 us (2%)
    reduce_scatter x1, waiting for transfers between devices, shards(): lax.psum_scatter(contract_last(delta_gate_up, forward_reduced), ('mlp', '...  146 us
    reduce_scatter x1, waiting for transfers between devices, shards(): lax.psum_scatter(jnp.dot(gated_low, mixer_low, preferred_element_type=jnp...  142 us
    reduce_scatter x1, waiting for transfers between devices, shards(): lax.psum_scatter(contract_last(delta_projected, attention_reduced).astype...  85.9 us
    all_gather x1, waiting for transfers between devices, shards(): lax.all_gather(normed_input.astype(jnp.bfloat16), ('mlp', 'head'), axis=0...  75.5 us
    all_gather x1, waiting for transfers between devices, shards(): lax.all_gather(normed_second.astype(jnp.bfloat16), ('mlp', 'head'), axis=...  75.4 us
    all_gather x1, waiting for transfers between devices, shards(): lax.all_gather(cotangent, ('mlp', 'head'), axis=0, tiled=True)  61.3 us
    all_gather x1, waiting for transfers between devices, shards(): lax.all_gather(delta_middle.astype(jnp.bfloat16), ('mlp', 'head'), axis=0...  59.6 us
    reduce_scatter x1, waiting for transfers between devices, shards(): lax.psum_scatter(output_gradient.astype(jnp.bfloat16), 'seq', scatter_dim...  44.8 us
  transfers between devices with their start and end apart: 14, of which 13 were waited for; matrix products, arithmetic and copies ran while one was open for 14% of the time, Pallas kernels for 0%

commit v1 on v0

--- a/solution.py
+++ b/solution.py
@@ -1,8 +1,11 @@
+import functools
 import math
 
 import jax
 import jax.numpy as jnp
 from jax import lax
+from jax.experimental import pallas as pl
+from jax.experimental.pallas import tpu as pltpu
 from jax.sharding import PartitionSpec as P
 
 norm_epsilon = 1e-06
@@ -14,6 +17,162 @@
 learn_rate = 0.3
 masked_score = -1e30
 highest_precision = lax.Precision.HIGHEST
+MESH = pl.DeviceIdType.MESH
+
+
+def remote(src, dst, ssem, rsem, dev):
+    return pltpu.make_async_remote_copy(src_ref=src, dst_ref=dst, send_sem=ssem, recv_sem=rsem, device_id=dev, device_id_type=MESH)
+
+def enter(Z, z, y):
+    bar = pltpu.get_barrier_semaphore()
+    pl.semaphore_signal(bar, inc=1, device_id={"head": 1 - y}, device_id_type=MESH)
+    @pl.when(z > 0)
+    def _():
+        pl.semaphore_signal(bar, inc=1, device_id={"mlp": z - 1}, device_id_type=MESH)
+    @pl.when(z < Z - 1)
+    def _():
+        pl.semaphore_signal(bar, inc=1, device_id={"mlp": z + 1}, device_id_type=MESH)
+    inner = (z > 0) & (z < Z - 1)
+    @pl.when(inner)
+    def _(): pl.semaphore_wait(bar, 3)
+    @pl.when(jnp.logical_not(inner))
+    def _(): pl.semaphore_wait(bar, 2)
+
+def ag_kernel(Z, C, x_ref, out_ref, usem, dsem, ysem, rsem):
+    z = lax.axis_index("mlp"); y = lax.axis_index("head")
+    R = x_ref.shape[0]; r = R // C
+    enter(Z, z, y)
+    own = z * 2 + y
+    def cp(src, b, c, sem, dev):
+        return remote(src, out_ref.at[b, pl.ds(c * r, r)], sem, rsem.at[b, c], dev)
+    def blk(b, c): return out_ref.at[b, pl.ds(c * r, r)]
+    def up(src, b, zb, c): return cp(src, b, c, usem.at[zb, c], {"mlp": z + 1})
+    def dn(src, b, zb, c): return cp(src, b, c, dsem.at[zb, c], {"mlp": z - 1})
+    def yy(src, b, zb, c): return cp(src, b, c, ysem.at[zb, c], {"head": 1 - y})
+    for c in range(C):
+        s = x_ref.at[pl.ds(c * r, r)]
+        @pl.when(z < Z - 1)
+        def _(): up(s, own, z, c).start()
+        @pl.when(z > 0)
+        def _(): dn(s, own, z, c).start()
+        yy(s, own, z, c).start()
+    out_ref[own] = x_ref[...]
+    for k in range(1, Z):
+        for c in range(C):
+            @pl.when(z - k >= 0)
+            def _():
+                zb = z - k; b = zb * 2 + y
+                yy(blk(b, c), b, zb, c).wait_recv()
+                @pl.when(z < Z - 1)
+                def _(): up(blk(b, c), b, zb, c).start()
+                yy(blk(b, c), b, zb, c).start()
+            @pl.when(z + k <= Z - 1)
+            def _():
+                zb = z + k; b = zb * 2 + y
+                yy(blk(b, c), b, zb, c).wait_recv()
+                @pl.when(z > 0)
+                def _(): dn(blk(b, c), b, zb, c).start()
+                yy(blk(b, c), b, zb, c).start()
+    for zb in range(Z):
+        for c in range(C):
+            b = zb * 2 + (1 - y)
+            yy(blk(b, c), b, zb, c).wait_recv()
+    for zb in range(Z):
+        for c in range(C):
+            b = zb * 2 + y
+            yy(blk(b, c), b, zb, c).wait_send()
+            @pl.when((z < Z - 1) & (zb <= z))
+            def _(): up(blk(b, c), b, zb, c).wait_send()
+            @pl.when((z > 0) & (zb >= z))
+            def _(): dn(blk(b, c), b, zb, c).wait_send()
+
+def ag(x, Z, C, cid=1):
+    R, D = x.shape
+    return pl.pallas_call(functools.partial(ag_kernel, Z, C),
+        out_shape=jax.ShapeDtypeStruct((2 * Z, R, D), x.dtype),
+        in_specs=[pl.BlockSpec(memory_space=pltpu.VMEM)], out_specs=pl.BlockSpec(memory_space=pltpu.VMEM),
+        scratch_shapes=[pltpu.SemaphoreType.DMA((Z, C))] * 3 + [pltpu.SemaphoreType.DMA((2 * Z, C))],
+        compiler_params=pltpu.CompilerParams(collective_id=cid, has_side_effects=True, vmem_limit_bytes=60 << 20))(x)
+
+def rs_kernel(Z, C, p_ref, out_ref, ybuf, bbuf, abuf, ubuf, dbuf, ysem, usem, dsem, yr, br, ar):
+    z = lax.axis_index("mlp"); y = lax.axis_index("head")
+    R, D = out_ref.shape; r = R // C
+    enter(Z, z, y)
+    def rows(c): return pl.ds(c * r, r)
+    def yy(zb, c): return remote(p_ref.at[zb * 2 + 1 - y, rows(c)], ybuf.at[zb, rows(c)], ysem.at[zb, c], yr.at[zb, c], {"head": 1 - y})
+    def up(zb, c): return remote(ubuf.at[zb, rows(c)], bbuf.at[zb, rows(c)], usem.at[zb, c], br.at[zb, c], {"mlp": z + 1})
+    def dn(zb, c): return remote(dbuf.at[zb, rows(c)], abuf.at[zb, rows(c)], dsem.at[zb, c], ar.at[zb, c], {"mlp": z - 1})
+    for k in range(Z - 1, -1, -1):
+        for c in range(C):
+            @pl.when(z + k <= Z - 1)
+            def _(): yy(z + k, c).start()
+            if k:
+                @pl.when(z - k >= 0)
+                def _(): yy(z - k, c).start()
+    f = lambda v: v.astype(jnp.float32)
+    def own(zb, c): return f(p_ref[zb * 2 + y, rows(c)]) + f(ybuf[zb, rows(c)])
+    for k in range(Z - 1, 0, -1):
+        for c in range(C):
+            @pl.when(z + k <= Z - 1)
+            def _():
+                zb = z + k
+                yy(zb, c).wait_recv()
+                @pl.when(z > 0)
+                def _():
+                    up(zb, c).wait_recv()
+                    ubuf[zb, rows(c)] = (own(zb, c) + f(bbuf[zb, rows(c)])).astype(ubuf.dtype)
+                @pl.when(z == 0)
+                def _():
+                    ubuf[zb, rows(c)] = own(zb, c).astype(ubuf.dtype)
+                up(zb, c).start()
+            @pl.when(z - k >= 0)
+            def _():
+                zb = z - k
+                yy(zb, c).wait_recv()
+                @pl.when(z < Z - 1)
+                def _():
+                    dn(zb, c).wait_recv()
+                    dbuf[zb, rows(c)] = (own(zb, c) + f(abuf[zb, rows(c)])).astype(dbuf.dtype)
+                @pl.when(z == Z - 1)
+                def _():
+                    dbuf[zb, rows(c)] = own(zb, c).astype(dbuf.dtype)
+                dn(zb, c).start()
+    for c in range(C):
+        yy(z, c).wait_recv()
+        out_ref[rows(c)] = own(z, c)
+        @pl.when(z > 0)
+        def _():
+            up(z, c).wait_recv()
+            out_ref[rows(c)] += f(bbuf[z, rows(c)])
+        @pl.when(z < Z - 1)
+        def _():
+            dn(z, c).wait_recv()
+            out_ref[rows(c)] += f(abuf[z, rows(c)])
+    for zb in range(Z):
+        for c in range(C):
+            yy(zb, c).wait_send()
+            @pl.when(zb > z)
+            def _(): up(zb, c).wait_send()
+            @pl.when(zb < z)
+            def _(): dn(zb, c).wait_send()
+
+def rs(p, Z, C, cid=2):
+    _, R, D = p.shape
+    return pl.pallas_call(functools.partial(rs_kernel, Z, C),
+        out_shape=jax.ShapeDtypeStruct((R, D), jnp.float32),
+        in_specs=[pl.BlockSpec(memory_space=pltpu.VMEM)], out_specs=pl.BlockSpec(memory_space=pltpu.VMEM),
+        scratch_shapes=[pltpu.VMEM((Z, R, D), p.dtype)] * 5 + [pltpu.SemaphoreType.DMA((Z, C))] * 6,
+        compiler_params=pltpu.CompilerParams(collective_id=cid, has_side_effects=True, vmem_limit_bytes=60 << 20))(p)
+
+
+def gather_rows(rows, cid):
+    full = ag(rows, lax.axis_size("mlp"), 2, cid)
+    return full.reshape(-1, rows.shape[1])
+
+
+def scatter_rows(partial, cid):
+    levels = lax.axis_size("mlp")
+    return rs(partial.reshape(2 * levels, -1, partial.shape[1]), levels, 2, cid)
 
 
 def scaled_norm(values, norm_gain):
@@ -189,9 +348,7 @@
     cosine_table, sine_table = rotary_tables(position, head_width)
     inputs = tokens.astype(jnp.float32)
     normed_input, back_one = jax.vjp(scaled_norm, inputs, gain_one)
-    normed_rows = lax.all_gather(
-        normed_input.astype(jnp.bfloat16), ("mlp", "head"), axis=0, tiled=True
-    )
+    normed_rows = gather_rows(normed_input.astype(jnp.bfloat16), 1)
     projected_rows = jnp.dot(normed_rows, attention_reduced, preferred_element_type=jnp.float32)
     query_rows = projected_rows[:, :query_cols].reshape(total_rows, query_heads, head_width)
     keys_raw = projected_rows[:, query_cols : query_cols + head_width]
@@ -234,17 +391,12 @@
     attended_rows = jnp.concatenate(pieces, axis=0).reshape(total_rows, query_cols)
     gate_sigmoid = jax.nn.sigmoid(gate_scores_raw)
     gated_low = (attended_rows * gate_sigmoid).astype(jnp.bfloat16)
-    attention_out = lax.psum_scatter(
-        jnp.dot(gated_low, mixer_low, preferred_element_type=jnp.float32),
-        ("mlp", "head"),
-        scatter_dimension=0,
-        tiled=True,
+    attention_out = scatter_rows(
+        jnp.dot(gated_low, mixer_low, preferred_element_type=jnp.float32).astype(jnp.bfloat16), 2
     )
     middle = inputs + attention_out
     normed_second, back_two = jax.vjp(scaled_norm, middle, gain_two)
-    feed_rows = lax.all_gather(
-        normed_second.astype(jnp.bfloat16), ("mlp", "head"), axis=0, tiled=True
-    )
+    feed_rows = gather_rows(normed_second.astype(jnp.bfloat16), 3)
     gate_up_product = jnp.dot(feed_rows, forward_reduced, preferred_element_type=jnp.float32)
     activated, back_swiglu = jax.vjp(swiglu, gate_up_product)
     activated_low = activated.astype(jnp.bfloat16)
@@ -260,17 +412,12 @@
     delta_gate_up = back_swiglu(delta_activated)[0].astype(jnp.bfloat16)
     down_gradient = contract_first(activated_low, cotangent_rows)
     feed_gradient = contract_first(feed_rows, delta_gate_up)
-    delta_normed_two = lax.psum_scatter(
-        contract_last(delta_gate_up, forward_reduced),
-        ("mlp", "head"),
-        scatter_dimension=0,
-        tiled=True,
+    delta_normed_two = scatter_rows(
+        contract_last(delta_gate_up, forward_reduced).astype(jnp.bfloat16), 4
     )
     delta_middle_part, delta_gain_two = back_two(delta_normed_two)
     delta_middle = cotangent.astype(jnp.float32) + delta_middle_part
-    branch_rows = lax.all_gather(
-        delta_middle.astype(jnp.bfloat16), ("mlp", "head"), axis=0, tiled=True
-    )
+    branch_rows = gather_rows(delta_middle.astype(jnp.bfloat16), 5)
     delta_gated = contract_last(branch_rows, mixer_low)
     mixer_gradient = contract_first(gated_low, branch_rows)
     delta_attended = delta_gated * gate_sigmoid
@@ -317,12 +464,9 @@
     delta_projected = jnp.concatenate(
         [query_back.reshape(total_rows, query_cols), key_back, value_delta, delta_logits], axis=1
     ).astype(jnp.bfloat16)
-    delta_normed = lax.psum_scatter(
-        contract_last(delta_projected, attention_reduced).astype(jnp.bfloat16),
-        ("mlp", "head"),
-        scatter_dimension=0,
-        tiled=True,
-    ).astype(jnp.float32)
+    delta_normed = scatter_rows(
+        contract_last(delta_projected, attention_reduced).astype(jnp.bfloat16), 6
+    )
     delta_input_part, delta_gain_one = back_one(delta_normed)
     input_gradient = delta_middle + delta_input_part
     attention_gradient = contract_first(normed_rows, delta_projected)

time: 1100 us -> 702 us (0.64)
  waiting for transfers between devices: 831 us -> 131 us
  Pallas kernels: 0 us -> 320 us
    reduce_scatter x3 -> x0, waiting for transfers between devices: 374 us -> none  [the longest x1 146 us: shards(): lax.psum_scatter(contract_last(delta_gate_up, forward_reduced), ('mlp', '...]
    pallas_call x0 -> x6, Pallas kernels: none -> 320 us  [the longest x3 169 us: ag(): pl.pallas_call(functools.partial(ag_kernel, Z, C), out_shape=jax.ShapeDty...]
    all_gather x3 -> x0, waiting for transfers between devices: 210 us -> none  [the longest x1 75.5 us: shards(): lax.all_gather(normed_input.astype(jnp.bfloat16), ('mlp', 'head'), axis=0...]
    all_gather x1, waiting for transfers between devices: 61.3 us -> 0.01 us  [shards(): lax.all_gather(cotangent, ('mlp', 'head'), axis=0, tiled=True)]
    reduce_scatter x1, waiting for transfers between devices: 30.4 us -> 84.7 us  [shards(): lax.psum_scatter(jnp.dot(activated_low, down_low, preferred_element_type=...]
    reduce_scatter x1, waiting for transfers between devices: 0.02 us -> 45.2 us  [shards(): lax.psum_scatter(feed_gradient.astype(jnp.bfloat16), 'seq', scatter_dimen...]
    reduce_scatter x1, waiting for transfers between devices: 44.8 us -> 0.02 us  [shards(): lax.psum_scatter(output_gradient.astype(jnp.bfloat16), 'seq', scatter_dim...]
    all_gather x1, waiting for transfers between devices: 44 us -> 0.02 us  [shards(): lax.all_gather(feedforward_in.astype(jnp.bfloat16), 'seq', axis=0, tiled=...]
  transfers between devices with their start and end apart: 14 -> 8, of which waited for: 13 -> 2; matrix products, arithmetic and copies ran while one was open for 14% -> 16% of each run, Pallas kernels for 0% -> 33%
where the time goes in v1:
time: 702 us; the launch traced here: 696 us
  Pallas kernels  320 us (46%)
  waiting for transfers between devices  131 us (19%)
  matrix products  108 us (15%)
  other arithmetic  72.2 us (10%)
  blocking collectives  40.5 us (6%)
  between operations  16.1 us (2%)
  local copies, waits for them, and re-layouts  8.23 us (1%)
    pallas_call x3, Pallas kernels, ag(): pl.pallas_call(functools.partial(ag_kernel, Z, C), out_shape=jax.ShapeDty...  169 us
    pallas_call x3, Pallas kernels, rs(): pl.pallas_call(functools.partial(rs_kernel, Z, C), out_shape=jax.ShapeDty...  151 us
    reduce_scatter x1, waiting for transfers between devices, shards(): lax.psum_scatter(jnp.dot(activated_low, down_low, preferred_element_type=...  84.7 us
    reduce_scatter x1, waiting for transfers between devices, shards(): lax.psum_scatter(feed_gradient.astype(jnp.bfloat16), 'seq', scatter_dimen...  45.2 us
    psum x1, blocking collectives, shards(): lax.psum((gain_local, norm_local), ('seq', 'mlp', 'head'))  40.5 us
    dot_general x4, matrix products, contract_last(): lax.dot_general(left, right, (((1,), (1,)), ((), ())), preferred_element_...  30.9 us
    reduce_sum x6, other arithmetic, kind_sums(): jnp.sum(matrix * matrix, axis=over_axis)  27.2 us
    dot_general x4, matrix products, contract_first(): lax.dot_general(left, right, (((0,), (0,)), ((), ())), preferred_element_...  24.3 us
  transfers between devices with their start and end apart: 8, of which 2 were waited for; matrix products, arithmetic and copies ran while one was open for 16% of the time, Pallas kernels for 33%

profile of v1, /device:TPU:0, one launch (start us, length us, event | category | flops | bytes accessed | tf_op | source)
XLA Modules:
  0.0 695.6 jit_solution(4899760422834656620)
XLA Ops:
  7.2 3.1 multiply_reduce_fusion.5
  10.4 3.6 multiply_reduce_fusion.3
  14.1 1.4 multiply_reduce_fusion.1
  16.2 1.2 fusion.40
  17.4 2.0 fusion.35.x_ref
  19.5 53.4 %shard_map.305 = bf16[8,128,2048]{2,1,0:T(8,128)(2,1)} custom-call(bf16[128,2048]{1,0:T(8,128)(2,1)} %fusion.35.x_ref), custom_call_target="tpu_custom_call" | custom-call | tf_op jit(solution)/shard_map/pallas_call | solution.py:91
  74.6 8.1 %fusion.137 = (bf16[1024,768]{0,1:T(8,128)(2,1)}, f32[1024,768]{0,1:T(8,128)S(1)}) fusion(bf16[1024,2048]{1,0:T(8,128)(2,1)} %bitcast.186, bf16[2048,768]{1,0:T(8,128)(2,1)} %all-gather.5.cloned.1.call-done), kind=kOutput, calls=%fused_computation.261 | convolution fusion | flops 3222011904 | bytes 12058624 | tf_op jit(solution)/shard_map/dot_general | solution.py:352
  82.9 1.5 fusion.71
  84.4 1.1 slice.191
  85.9 1.9 copy.58
  87.7 1.8 multiply_reduce_fusion.11
  91.9 1.0 fusion.12
  93.0 1.0 exponential_reduce_fusion
  94.0 1.6 convolution_bitcast_fusion.3
  95.6 2.3 convolution_bitcast_fusion.2
  98.0 1.0 copy-done.27
  98.9 1.6 fusion.45
  100.5 4.7 convolution_convert_fusion.2
  105.2 57.4 %shard_map.306 = f32[128,2048]{1,0:T(8,128)} custom-call(bf16[8,128,2048]{2,1,0:T(8,128)(2,1)} %bitcast.183), custom_call_target="tpu_custom_call" | custom-call | tf_op jit(solution)/shard_map/pallas_call | solution.py:161
  162.6 1.4 multiply_reduce_fusion.10
  164.1 1.1 multiply_convert_fusion.2.x_ref
  165.2 71.0 %shard_map.307 = bf16[8,128,2048]{2,1,0:T(8,128)(2,1)} custom-call(bf16[128,2048]{1,0:T(8,128)(2,1)} %multiply_convert_fusion.2.x_ref), custom_call_target="tpu_custom_call" | custom-call | tf_op jit(solution)/shard_map/pallas_call | solution.py:91
  236.2 12.2 %fusion.139 = f32[1024,1536]{1,0:T(8,128)} fusion(bf16[1024,2048]{1,0:T(8,128)(2,1)} %bitcast.188, bf16[2048,1536]{1,0:T(8,128)(2,1)} %all-gather.9.cloned.1.call-done), kind=kOutput, calls=%fused_computation.263 | convolution fusion | flops 6442450944 | bytes 16777216 | tf_op jit(solution)/shard_map/dot_general | solution.py:400
  248.4 10.6 %fusion.66 = (f32[1024,768]{1,0:T(8,128)S(1)}, f32[1024,768]{1,0:T(8,128)S(1)}, bf16[1024,768]{1,0:T(8,128)(2,1)}) fusion(f32[1024,1536]{1,0:T(8,128)} %fusion.139, bf16[1024,2048]{1,0:T(8,128)(2,1)} %all-gather.11.cloned.1.call-done, bf16[1024,2048]{1,0:T(8,128)(2,1)} %all-gather.7.cloned.1.call-done), kind=kOutput, calls=%fused_computation.168 | convolution fusion | flops 3232235520 | bytes 21495808 | tf_op jit(solution)/shard_map/dot_general | solution.py:274
  259.0 8.3 %convolution_convert_fusion.1 = bf16[1024,2048]{1,0:T(8,128)(2,1)} fusion(bf16[2048,1536]{1,0:T(8,128)(2,1)S(1)} %copy-done.44, f32[1024,768]{1,0:T(8,128)S(1)} %get-tuple-element.118, f32[1024,768]{1,0:T(8,128)S(1)} %get-tuple-element.117), kind=kOutput, calls=%fused_computation.14 | convolution fusion | flops 6447693824 | bytes 16777216 | tf_op jit(solution)/shard_map/dot_general | solution.py:274
  267.3 46.0 %shard_map.308 = f32[128,2048]{1,0:T(8,128)} custom-call(bf16[8,128,2048]{2,1,0:T(8,128)(2,1)} %bitcast.185), custom_call_target="tpu_custom_call" | custom-call | tf_op jit(solution)/shard_map/pallas_call | solution.py:161
  313.3 1.5 multiply_reduce_fusion.7
  314.8 2.4 fusion.122.x_ref
  317.2 44.4 %shard_map.309 = bf16[8,128,2048]{2,1,0:T(8,128)(2,1)} custom-call(bf16[128,2048]{1,0:T(8,128)(2,1)} %fusion.122.x_ref), custom_call_target="tpu_custom_call" | custom-call | tf_op jit(solution)/shard_map/pallas_call | solution.py:91
  361.6 5.0 multiply_convert_fusion.1
  366.7 1.5 fusion.15
  369.4 1.3 fusion.30
  370.7 1.2 convolution_bitcast_fusion.4
  371.9 2.5 fusion
  374.4 1.3 fusion.2
  375.7 0.9 fusion.27
  377.5 0.9 multiply_reduce_fusion.6
  378.5 1.2 fusion.38
  379.7 1.0 copy.75
  380.7 1.9 fusion.26
  382.6 1.2 fusion.74
  383.8 1.2 multiply_reduce_fusion.12
  385.0 1.2 fusion.53
  386.3 1.4 fusion.29
  388.7 4.9 convolution_convert_fusion.6
  393.7 1.0 copy-done.30
  394.6 3.6 convolution_convert_fusion.7
  398.3 3.7 convolution_convert_fusion.5
  402.0 2.3 pad_maximum_fusion
  404.4 12.2 %convolution_convert_fusion = bf16[2048,1536]{1,0:T(8,128)(2,1)} fusion(bf16[1024,2048]{1,0:T(8,128)(2,1)} %bitcast.189, f32[1024,768]{1,0:T(8,128)} %copy-done.50, f32[1024,768]{1,0:T(8,128)} %copy-done.49), kind=kOutput, calls=%fused_computation | convolution fusion | flops 6448742400 | bytes 16777216 | tf_op jit(solution)/shard_map/dot_general | solution.py:268
  416.6 7.2 %convolution_convert_fusion.4 = bf16[1024,2048]{1,0:T(8,128)(2,1)} fusion(bf16[1024,768]{1,0:T(8,128)(2,1)S(1)} %copy-done.46, bf16[1024,2048]{1,0:T(8,128)(2,1)} %all-gather.7.cloned.1.call-done), kind=kOutput, calls=%fused_computation.17 | convolution fusion | flops 3223322624 | bytes 8912896 | tf_op jit(solution)/shard_map/dot_general | solution.py:404
  425.9 7.0 %convolution_convert_fusion.3 = bf16[1024,2048]{1,0:T(8,128)(2,1)} fusion(bf16[2048,768]{1,0:T(8,128)(2,1)} %all-gather.5.cloned.1.call-done, bf16[1024,256]{0,1:T(8,128)(2,1)S(1)} %copy-done.48, bf16[1024,128]{0,1:T(8,128)(2,1)S(1)} %fusion.29, bf16[1024,128]{0,1:T(8,128)(2,1)S(1)} %fusion.53, bf16[1024,256]{0,1:T(8,128)(2,1)S(1)} %bitcast.198), kind=kOutput, calls=%fused_computation.16 | convolution fusion | flops 3229614080 | bytes 8912896 | tf_op jit(solution)/shard_map/dot_general | solution.py:274
  432.9 47.4 %shard_map.310 = f32[128,2048]{1,0:T(8,128)} custom-call(bf16[8,128,2048]{2,1,0:T(8,128)(2,1)} %bitcast.184), custom_call_target="tpu_custom_call" | custom-call | tf_op jit(solution)/shard_map/pallas_call | solution.py:161
  480.4 1.6 fusion.36
  482.1 4.6 multiply_reduce_fusion.4
  487.0 7.9 %multiply_reduce_fusion.2 = (f32[1024]{0:T(1024)S(1)}, f32[1024,512]{1,0:T(8,128)}, f32[1024,512]{1,0:T(8,128)}, f32[1024,512]{1,0:T(8,128)}) fusion(f32[1024,512]{1,0:T(8,128)} %param.32, f32[]{:T(128)} %bitcast.39, f32[]{:T(128)} %bitcast.38, bf16[1024,512]{1,0:T(8,128)(2,1)} %reduce-scatter.11.cloned.1.call-done, f32[1024,512]{1,0:T(8,128)} %param.38, ...), kind=kLoop, calls=%fused_computation.49 | loop fusion | flops 8387584 | bytes 13635592 | tf_op jit(solution)/shard_map/reduce_sum | solution.py:246
  495.2 45.2 %reduce-scatter.9.cloned.1.call-done = bf16[512,1536]{1,0:T(8,128)(2,1)} async-done(((bf16[2048,1536]{1,0:T(8,128)(2,1)}), bf16[512,1536]{1,0:T(8,128)(2,1)}) %reduce-scatter.9.cloned.1.call-update) | async-done | bytes 1572880 | tf_op jit(solution)/shard_map/reduce_scatter | solution.py:478
  540.5 6.7 multiply_reduce_fusion
  547.7 84.7 %reduce-scatter.5.cloned.1.call-done = bf16[128,2048]{1,0:T(8,128)(2,1)} async-done(((bf16[1024,2048]{1,0:T(8,128)(2,1)}), bf16[128,2048]{1,0:T(8,128)(2,1)}) %reduce-scatter.5.cloned.1.call-update) | async-done | bytes 524304 | tf_op jit(solution)/shard_map/reduce_scatter | solution.py:403
  632.5 3.9 fusion.39
  636.4 40.5 %all-reduce.8 = (f32[16]{0:T(128)S(1)}, f32[4352]{0:T(1024)S(1)}) all-reduce(f32[16]{0:T(128)S(1)} %pad_maximum_fusion.10, f32[4352]{0:T(1024)S(1)} %pad_maximum_fusion.8), channel_id=1, replica_groups=mesh['seq'=4,'mlp'=4,'head'=2] {'seq','mlp','head'}, use_global_device_ids=true, to_apply=%region_27.28 | all-reduce | flops 4368 | bytes 34944 | tf_op jit(solution)/shard_map/psum | solution.py:522
  679.0 4.3 fusion.124
  683.4 3.0 fusion.125
  686.3 1.6 fusion.126
  (180 shorter events, 14.2 us)
Async XLA Ops:
  7.2 6.9 copy-start.3
  7.2 67.4 %all-gather.5.cloned.1.call-start = ((), (), s32[]{:S(2)}) async-start(), calls=%async_computation.4 | async-start | bytes 3932160 | tf_op jit(solution)/shard_map/all_gather | solution.py:341
  10.3 90.2 %all-gather.7.cloned.1.call-start = ((), (), s32[]{:S(2)}) async-start(), calls=%async_computation.5 | async-start | bytes 5242880 | tf_op jit(solution)/shard_map/all_gather | solution.py:343
  14.0 2.1 copy-start.39
  14.0 222.2 %all-gather.9.cloned.1.call-start = ((), (), s32[]{:S(2)}) async-start(), calls=%async_computation.6 | async-start | bytes 7864320 | tf_op jit(solution)/shard_map/all_gather | solution.py:342
  15.5 232.9 %all-gather.11.cloned.1.call-start = ((), (), s32[]{:S(2)}) async-start(), calls=%async_computation.8 | async-start | bytes 4718592 | tf_op jit(solution)/shard_map/all_gather | solution.py:410
  16.1 466.0 %reduce-scatter.7.cloned.1.call-start = ((), (), s32[]{:S(2)}) async-start(), calls=%async_computation.9 | async-start | bytes 3932160 | tf_op jit(solution)/shard_map/reduce_scatter | solution.py:475
  16.2 56.7 %copy-start.43 = (s32[1,8]{1,0:T(1,128)S(1)}, s32[1,8]{1,0:T(1,128)}, u32[]{:S(2)}) copy-start(s32[1,8]{1,0:T(1,128)} %param.42) | copy-start | bytes 100
  74.6 21.0 %copy-start.14 = (pred[512,1024]{0,1:T(8,128)(4,1)}, pred[512,1024]{0,1:T(8,128)(4,1)S(1)}, u32[]{:S(2)}) copy-start(pred[512,1024]{0,1:T(8,128)(4,1)S(1)} %fusion.18) | copy-start | bytes 1572868
  82.7 1.7 copy-start.13
  85.6 4.7 copy-start.22
  85.8 4.5 copy-start.24
  87.7 2.7 copy-start.6
  89.9 1.0 copy-start.34
  90.4 1.5 copy-start.16
  90.4 1.5 copy-start.18
  90.6 2.4 copy-start.32
  93.0 2.6 copy-start
  98.0 1.0 copy-start.27
  100.5 4.7 copy-start.29
  105.2 57.4 %copy-start.10 = (bf16[128,2048]{1,0:T(8,128)(2,1)S(1)}, bf16[128,2048]{1,0:T(8,128)(2,1)}, u32[]{:S(2)}) copy-start(bf16[128,2048]{1,0:T(8,128)(2,1)} %param.28) | copy-start | bytes 1572868
  164.1 150.7 %copy-start.5 = (f32[128,2048]{1,0:T(8,128)}, f32[128,2048]{1,0:T(8,128)S(1)}, u32[]{:S(2)}) copy-start(f32[128,2048]{1,0:T(8,128)S(1)} %get-tuple-element.116) | copy-start | bytes 3145732
  248.4 10.6 %copy-start.44 = (bf16[2048,1536]{1,0:T(8,128)(2,1)S(1)}, bf16[2048,1536]{1,0:T(8,128)(2,1)}, u32[]{:S(2)}) copy-start(bf16[2048,1536]{1,0:T(8,128)(2,1)} %all-gather.9.cloned.1.call-done) | copy-start | bytes 18874372
  259.0 8.3 %copy-start.49 = (f32[1024,768]{1,0:T(8,128)}, f32[1024,768]{1,0:T(8,128)S(1)}, u32[]{:S(2)}) copy-start(f32[1024,768]{1,0:T(8,128)S(1)} %get-tuple-element.117) | copy-start | bytes 9437188
  259.0 8.3 %copy-start.50 = (f32[1024,768]{1,0:T(8,128)}, f32[1024,768]{1,0:T(8,128)S(1)}, u32[]{:S(2)}) copy-start(f32[1024,768]{1,0:T(8,128)S(1)} %get-tuple-element.118) | copy-start | bytes 9437188
  267.3 47.5 %copy-start.21 = (bf16[128,2048]{1,0:T(8,128)(2,1)S(1)}, bf16[128,2048]{1,0:T(8,128)(2,1)}, u32[]{:S(2)}) copy-start(bf16[128,2048]{1,0:T(8,128)(2,1)} %param.29) | copy-start | bytes 1572868
  317.2 44.4 %copy-start.28 = (f32[1024,2,128]{0,2,1:T(8,128)S(1)}, f32[1024,2,128]{0,2,1:T(8,128)}, u32[]{:S(2)}) copy-start(f32[1024,2,128]{0,2,1:T(8,128)} %copy-done.27) | copy-start | bytes 3145732
  366.7 5.2 copy-start.35
  368.2 1.2 copy-start.17
  368.2 1.2 copy-start.19
  368.8 3.1 copy-start.1
  368.8 3.1 copy-start.15
  375.7 1.0 copy-start.23
  375.7 1.2 copy-start.25
  375.7 1.8 copy-start.7
  378.4 2.3 copy-start.33
  380.7 5.5 copy-start.2
  380.7 5.5 copy-start.36
  380.7 5.5 copy-start.38
  386.2 2.2 copy-start.26
  386.2 2.3 copy-start.37
  386.3 2.4 copy-start.47
  393.6 1.0 copy-start.30
  393.6 4.6 copy-start.46
  393.6 93.4 %reduce-scatter.11.cloned.1.call-start = ((), (), s32[]{:S(2)}) async-start(), calls=%async_computation.11 | async-start | bytes 5242880 | tf_op jit(solution)/shard_map/reduce_scatter | solution.py:481
  394.6 3.6 copy-start.45
  404.3 136.2 %reduce-scatter.9.cloned.1.call-start = ((), (), s32[]{:S(2)}) async-start(), calls=%async_computation.10 | async-start | bytes 7864320 | tf_op jit(solution)/shard_map/reduce_scatter | solution.py:478
  416.5 215.9 %reduce-scatter.5.cloned.1.call-start = ((), (), s32[]{:S(2)}) async-start(), calls=%async_computation.7 | async-start | bytes 4718592 | tf_op jit(solution)/shard_map/reduce_scatter | solution.py:403
  423.8 2.1 copy-start.48
  432.9 47.5 %copy-start.11 = (bf16[128,2048]{1,0:T(8,128)(2,1)S(1)}, bf16[128,2048]{1,0:T(8,128)(2,1)}, u32[]{:S(2)}) copy-start(bf16[128,2048]{1,0:T(8,128)(2,1)} %param.28) | copy-start | bytes 1572868
  432.9 49.2 %copy-start.8 = (f32[512,768]{1,0:T(8,128)S(1)}, f32[512,768]{1,0:T(8,128)}, u32[]{:S(2)}) copy-start(f32[512,768]{1,0:T(8,128)} %param.30) | copy-start | bytes 4718596
  432.9 49.2 %copy-start.31 = (f32[512,768]{1,0:T(8,128)S(1)}, f32[512,768]{1,0:T(8,128)}, u32[]{:S(2)}) copy-start(f32[512,768]{1,0:T(8,128)} %param.36) | copy-start | bytes 4718596
  487.0 53.5 %copy-start.4 = (f32[512,1536]{1,0:T(8,128)S(1)}, f32[512,1536]{1,0:T(8,128)}, u32[]{:S(2)}) copy-start(f32[512,1536]{1,0:T(8,128)} %param.31) | copy-start | bytes 9437188
  679.0 4.3 copy-start.12
  683.3 3.0 copy-start.9
  683.3 3.0 copy-start.20
  686.3 1.6 copy-start.40
  686.3 1.6 copy-start.41
  686.3 1.6 copy-start.42
Sparse Core Ops, SparseCore 0:
  10.4 31.2 all-gather.4
  43.8 34.4 all-gather.6
  80.5 46.3 all-gather.8
  128.8 106.7 all-gather.10
  393.7 38.4 reduce-scatter.6
  434.6 44.3 reduce-scatter.10
  481.6 58.8 reduce-scatter.8
  544.1 88.2 reduce-scatter.4

commit v2 on v1

--- a/solution.py
+++ b/solution.py
@@ -165,6 +165,71 @@
         compiler_params=pltpu.CompilerParams(collective_id=cid, has_side_effects=True, vmem_limit_bytes=60 << 20))(p)
 
 
+def total_kernel(axes, x_ref, out_ref, *scratch):
+    count = len(axes)
+    slots, sums, send_sems, recv_sems = (scratch[i * count : (i + 1) * count] for i in range(4))
+    barrier = pltpu.get_barrier_semaphore()
+    for name, size in axes:
+        me = lax.axis_index(name)
+        for step in range(1, size):
+            pl.semaphore_signal(
+                barrier, inc=1, device_id={name: lax.rem(me + step, size)}, device_id_type=MESH
+            )
+    pl.semaphore_wait(barrier, sum(size - 1 for _, size in axes))
+    current = x_ref
+    for index, (name, size) in enumerate(axes):
+        me = lax.axis_index(name)
+
+        def copy(step):
+            return remote(
+                current,
+                slots[index].at[me],
+                send_sems[index].at[step],
+                recv_sems[index].at[me],
+                {name: lax.rem(me + step, size)},
+            )
+
+        def arrival(step):
+            source = lax.rem(me + size - step, size)
+            return remote(
+                current,
+                slots[index].at[source],
+                send_sems[index].at[step],
+                recv_sems[index].at[source],
+                {name: lax.rem(me + step, size)},
+            )
+
+        for step in range(1, size):
+            copy(step).start()
+        slots[index][me] = current[...]
+        for step in range(1, size):
+            arrival(step).wait_recv()
+        for step in range(1, size):
+            copy(step).wait_send()
+        total = slots[index][0]
+        for slot in range(1, size):
+            total = total + slots[index][slot]
+        if index == count - 1:
+            out_ref[...] = total
+        else:
+            sums[index][...] = total
+            current = sums[index]
+
+
+def total_over(values, axes, cid):
+    shape = values.shape
+    return pl.pallas_call(
+        functools.partial(total_kernel, axes),
+        out_shape=jax.ShapeDtypeStruct(shape, values.dtype),
+        in_specs=[pl.BlockSpec(memory_space=pltpu.VMEM)],
+        out_specs=pl.BlockSpec(memory_space=pltpu.VMEM),
+        scratch_shapes=[pltpu.VMEM((size, *shape), values.dtype) for _, size in axes]
+        + [pltpu.VMEM(shape, values.dtype) for _ in axes]
+        + [pltpu.SemaphoreType.DMA((size,)) for _, size in axes] * 2,
+        compiler_params=pltpu.CompilerParams(collective_id=cid, has_side_effects=True),
+    )(values)
+
+
 def gather_rows(rows, cid):
     full = ag(rows, lax.axis_size("mlp"), 2, cid)
     return full.reshape(-1, rows.shape[1])
@@ -400,26 +465,44 @@
     gate_up_product = jnp.dot(feed_rows, forward_reduced, preferred_element_type=jnp.float32)
     activated, back_swiglu = jax.vjp(swiglu, gate_up_product)
     activated_low = activated.astype(jnp.bfloat16)
-    feed_out = lax.psum_scatter(
-        jnp.dot(activated_low, down_low, preferred_element_type=jnp.float32).astype(jnp.bfloat16),
-        ("mlp", "head"),
-        scatter_dimension=0,
-        tiled=True,
-    ).astype(jnp.float32)
-    block_output = (middle + feed_out).astype(jnp.bfloat16)
     cotangent_rows = lax.all_gather(cotangent, ("mlp", "head"), axis=0, tiled=True)
     delta_activated = contract_last(cotangent_rows, down_low)
     delta_gate_up = back_swiglu(delta_activated)[0].astype(jnp.bfloat16)
-    down_gradient = contract_first(activated_low, cotangent_rows)
-    feed_gradient = contract_first(feed_rows, delta_gate_up)
-    delta_normed_two = scatter_rows(
-        contract_last(delta_gate_up, forward_reduced).astype(jnp.bfloat16), 4
-    )
+    down_gradient, feed_gradient, feed_delta_partial = lax.optimization_barrier(
+        (
+            contract_first(activated_low, cotangent_rows).astype(jnp.bfloat16),
+            contract_first(feed_rows, delta_gate_up).astype(jnp.bfloat16),
+            contract_last(delta_gate_up, forward_reduced).astype(jnp.bfloat16),
+        )
+    )
+    feed_total = lax.psum_scatter(
+        feed_gradient, "seq", scatter_dimension=0, tiled=True
+    ).astype(jnp.float32)
+    down_total = lax.psum_scatter(
+        down_gradient, "seq", scatter_dimension=1, tiled=True
+    ).astype(jnp.float32)
+    delta_normed_two = scatter_rows(feed_delta_partial, 4)
     delta_middle_part, delta_gain_two = back_two(delta_normed_two)
     delta_middle = cotangent.astype(jnp.float32) + delta_middle_part
-    branch_rows = gather_rows(delta_middle.astype(jnp.bfloat16), 5)
+    branch_rows, feed_out_partial = lax.optimization_barrier(
+        (
+            gather_rows(delta_middle.astype(jnp.bfloat16), 5),
+            jnp.dot(activated_low, down_low, preferred_element_type=jnp.float32).astype(
+                jnp.bfloat16
+            ),
+        )
+    )
+    feed_out = lax.psum_scatter(
+        feed_out_partial, ("mlp", "head"), scatter_dimension=0, tiled=True
+    ).astype(jnp.float32)
+    block_output = (middle + feed_out).astype(jnp.bfloat16)
     delta_gated = contract_last(branch_rows, mixer_low)
-    mixer_gradient = contract_first(gated_low, branch_rows)
+    mixer_total = lax.psum_scatter(
+        contract_first(gated_low, branch_rows).astype(jnp.bfloat16),
+        "seq",
+        scatter_dimension=1,
+        tiled=True,
+    ).astype(jnp.float32)
     delta_attended = delta_gated * gate_sigmoid
     delta_logits = delta_gated * attended_rows * gate_sigmoid * (1.0 - gate_sigmoid)
     delta_attended_low = delta_attended.astype(jnp.bfloat16).reshape(
@@ -464,24 +547,19 @@
     delta_projected = jnp.concatenate(
         [query_back.reshape(total_rows, query_cols), key_back, value_delta, delta_logits], axis=1
     ).astype(jnp.bfloat16)
-    delta_normed = scatter_rows(
-        contract_last(delta_projected, attention_reduced).astype(jnp.bfloat16), 6
-    )
+    attention_gradient, delta_partial = lax.optimization_barrier(
+        (
+            contract_first(normed_rows, delta_projected).astype(jnp.bfloat16),
+            contract_last(delta_projected, attention_reduced).astype(jnp.bfloat16),
+        )
+    )
+    attention_total = lax.psum_scatter(
+        attention_gradient, "seq", scatter_dimension=0, tiled=True
+    ).astype(jnp.float32)
+    delta_normed = scatter_rows(delta_partial, 6)
     delta_input_part, delta_gain_one = back_one(delta_normed)
     input_gradient = delta_middle + delta_input_part
-    attention_gradient = contract_first(normed_rows, delta_projected)
-    output_gradient = jnp.concatenate([mixer_gradient, down_gradient], axis=0)
-    attention_total, feed_total, output_total = (
-        lax.psum_scatter(
-            attention_gradient.astype(jnp.bfloat16), "seq", scatter_dimension=0, tiled=True
-        ).astype(jnp.float32),
-        lax.psum_scatter(
-            feed_gradient.astype(jnp.bfloat16), "seq", scatter_dimension=0, tiled=True
-        ).astype(jnp.float32),
-        lax.psum_scatter(
-            output_gradient.astype(jnp.bfloat16), "seq", scatter_dimension=1, tiled=True
-        ).astype(jnp.float32),
-    )
+    output_total = jnp.concatenate([mixer_total, down_total], axis=0)
     steps_done = step_count[0].astype(jnp.float32)
     correct_one = 1.0 - jnp.power(beta_one, steps_done)
     correct_two = 1.0 - jnp.power(beta_two, steps_done)
@@ -519,7 +597,15 @@
     )
     gain_local = jnp.concatenate([delta_gain_one, delta_gain_two, delta_gain_query, delta_gain_key])
     norm_local = jnp.concatenate([weight_local, update_local])
-    gain_total, norm_total = lax.psum((gain_local, norm_local), ("seq", "mlp", "head"))
+    packed = jnp.concatenate([gain_local, norm_local])
+    packed_rows = -(-packed.shape[0] // 1024) * 8
+    packed_total = total_over(
+        jnp.pad(packed, (0, packed_rows * 128 - packed.shape[0])).reshape(packed_rows, 128),
+        tuple((name, lax.axis_size(name)) for name in ("seq", "mlp", "head")),
+        7,
+    ).reshape(-1)
+    gain_total = packed_total[: gain_local.shape[0]]
+    norm_total = packed_total[gain_local.shape[0] : packed.shape[0]]
     weight_squares = norm_total[:8]
     update_squares = norm_total[8:]
     trust_ratio = jnp.sqrt(weight_squares) / jnp.sqrt(update_squares)

time: 702 us -> 741 us (1.056)
  waiting for transfers between devices: 131 us -> 189 us
  blocking collectives: 40.5 us -> 0 us
  Pallas kernels: 320 us -> 336 us
    reduce_scatter x4 -> x5, waiting for transfers between devices: 130 us -> 186 us  [the longest x1 85.8 us: shards(): lax.psum_scatter(feed_out_partial, ('mlp', 'head'), scatter_dimension=0,...]
    psum x1 -> x0, blocking collectives: 40.5 us -> none  [shards(): lax.psum((gain_local, norm_local), ('seq', 'mlp', 'head'))]
    pallas_call x0 -> x1, Pallas kernels: none -> 13.7 us  [total_over(): pl.pallas_call(functools.partial(total_kernel, axes), out_shape=jax.Shape...]
    reduce_sum x6 -> x4, other arithmetic: 27.2 us -> 20.7 us  [kind_sums(): jnp.sum(matrix * matrix, axis=over_axis)]
  transfers between devices with their start and end apart: 8 -> 9, of which waited for: 2 -> 4; matrix products, arithmetic and copies ran while one was open for 16% -> 10% of each run, Pallas kernels for 33% -> 31%
where the time goes in v2:
time: 741 us; the launch traced here: 735 us
  Pallas kernels  336 us (45%)
  waiting for transfers between devices  189 us (26%)
  matrix products  114 us (15%)
  other arithmetic  67.3 us (9%)
  between operations  16 us (2%)
  local copies, waits for them, and re-layouts  12.3 us (2%)
    pallas_call x3, Pallas kernels, ag(): pl.pallas_call(functools.partial(ag_kernel, Z, C), out_shape=jax.ShapeDty...  171 us
    pallas_call x3, Pallas kernels, rs(): pl.pallas_call(functools.partial(rs_kernel, Z, C), out_shape=jax.ShapeDty...  151 us
    reduce_scatter x1, waiting for transfers between devices, shards(): lax.psum_scatter(feed_out_partial, ('mlp', 'head'), scatter_dimension=0,...  85.8 us
    reduce_scatter x1, waiting for transfers between devices, shards(): lax.psum_scatter(feed_gradient, 'seq', scatter_dimension=0, tiled=True)  57.1 us
    reduce_scatter x1, waiting for transfers between devices, shards(): lax.psum_scatter(down_gradient, 'seq', scatter_dimension=1, tiled=True)  40.9 us
    dot_general x4, matrix products, contract_last(): lax.dot_general(left, right, (((1,), (1,)), ((), ())), preferred_element_...  35.3 us
    dot_general x4, matrix products, contract_first(): lax.dot_general(left, right, (((0,), (0,)), ((), ())), preferred_element_...  23.1 us
    reduce_sum x4, other arithmetic, kind_sums(): jnp.sum(matrix * matrix, axis=over_axis)  20.7 us
  transfers between devices with their start and end apart: 9, of which 4 were waited for; matrix products, arithmetic and copies ran while one was open for 10% of the time, Pallas kernels for 31%

profile of v2, /device:TPU:0, one launch (start us, length us, event | category | flops | bytes accessed | tf_op | source)
XLA Modules:
  0.0 734.6 jit_solution(4755075249460581432)
XLA Ops:
  7.2 3.1 multiply_reduce_fusion.5
  10.4 2.7 convert_element_type.150
  13.2 1.3 convert_element_type.154
  15.2 1.2 fusion.40
  16.5 2.0 fusion.35.x_ref
  18.5 53.3 %shard_map.305 = bf16[8,128,2048]{2,1,0:T(8,128)(2,1)} custom-call(bf16[128,2048]{1,0:T(8,128)(2,1)} %fusion.35.x_ref), custom_call_target="tpu_custom_call" | custom-call | tf_op jit(solution)/shard_map/pallas_call | solution.py:91
  73.5 8.1 %fusion.139 = (bf16[1024,768]{0,1:T(8,128)(2,1)}, f32[1024,768]{0,1:T(8,128)S(1)}) fusion(bf16[1024,2048]{1,0:T(8,128)(2,1)} %bitcast.196, bf16[2048,768]{1,0:T(8,128)(2,1)} %all-gather.5.cloned.1.call-done), kind=kOutput, calls=%fused_computation.261 | convolution fusion | flops 3222011904 | bytes 12058624 | tf_op jit(solution)/shard_map/dot_general | solution.py:417
  81.8 1.4 fusion.71
  83.3 1.1 slice.202
  84.8 1.7 copy.58
  86.6 1.8 multiply_reduce_fusion.11
  90.7 1.0 fusion.12
  92.8 1.5 convolution_bitcast_fusion.3
  94.4 2.3 convolution_bitcast_fusion.2
  97.8 1.6 fusion.45
  99.4 4.6 convolution_convert_fusion.2
  104.0 57.0 %shard_map.306 = f32[128,2048]{1,0:T(8,128)} custom-call(bf16[8,128,2048]{2,1,0:T(8,128)(2,1)} %bitcast.193), custom_call_target="tpu_custom_call" | custom-call | tf_op jit(solution)/shard_map/pallas_call | solution.py:161
  161.0 1.4 multiply_reduce_fusion.10
  162.5 1.1 multiply_convert_fusion.2.x_ref
  163.6 71.9 %shard_map.307 = bf16[8,128,2048]{2,1,0:T(8,128)(2,1)} custom-call(bf16[128,2048]{1,0:T(8,128)(2,1)} %multiply_convert_fusion.2.x_ref), custom_call_target="tpu_custom_call" | custom-call | tf_op jit(solution)/shard_map/pallas_call | solution.py:91
  235.5 12.1 %fusion.141 = f32[1024,1536]{1,0:T(8,128)} fusion(bf16[1024,2048]{1,0:T(8,128)(2,1)} %bitcast.200, bf16[2048,1536]{1,0:T(8,128)(2,1)} %all-gather.9.cloned.1.call-done), kind=kOutput, calls=%fused_computation.263 | convolution fusion | flops 6442450944 | bytes 16777216 | tf_op jit(solution)/shard_map/dot_general | solution.py:465
  247.6 10.6 %fusion.66 = (f32[1024,768]{1,0:T(8,128)S(1)}, f32[1024,768]{1,0:T(8,128)S(1)}, bf16[1024,768]{1,0:T(8,128)(2,1)}) fusion(f32[1024,1536]{1,0:T(8,128)} %fusion.141, bf16[1024,2048]{1,0:T(8,128)(2,1)} %all-gather.11.cloned.1.call-done, bf16[1024,2048]{1,0:T(8,128)(2,1)} %all-gather.7.cloned.1.call-done), kind=kOutput, calls=%fused_computation.168 | convolution fusion | flops 3232235520 | bytes 21495808 | tf_op jit(solution)/shard_map/dot_general | solution.py:339
  258.2 1.7 copy-done.48
  259.8 1.0 copy-done.49
  260.9 8.9 %convolution_convert_fusion = bf16[2048,1536]{1,0:T(8,128)(2,1)} fusion(bf16[1024,2048]{1,0:T(8,128)(2,1)S(1)} %bitcast.201, f32[1024,768]{1,0:T(8,128)S(1)} %get-tuple-element.130, f32[1024,768]{1,0:T(8,128)S(1)} %get-tuple-element.129), kind=kOutput, calls=%fused_computation | convolution fusion | flops 6448742400 | bytes 16777216 | tf_op jit(solution)/shard_map/dot_general | solution.py:333
  269.8 12.7 %convolution_convert_fusion.1 = bf16[1024,2048]{1,0:T(8,128)(2,1)} fusion(bf16[2048,1536]{1,0:T(8,128)(2,1)} %all-gather.9.cloned.1.call-done, f32[1024,768]{1,0:T(8,128)} %copy-done.49, f32[1024,768]{1,0:T(8,128)} %copy-done.48), kind=kOutput, calls=%fused_computation.13 | convolution fusion | flops 6447693824 | bytes 16777216 | tf_op jit(solution)/shard_map/dot_general | solution.py:339
  282.5 4.8 convolution_convert_fusion.6
  287.4 47.2 %shard_map.308 = f32[128,2048]{1,0:T(8,128)} custom-call(bf16[8,128,2048]{2,1,0:T(8,128)(2,1)} %bitcast.195), custom_call_target="tpu_custom_call" | custom-call | tf_op jit(solution)/shard_map/pallas_call | solution.py:161
  334.6 1.5 multiply_reduce_fusion.7
  336.1 2.4 fusion.123.x_ref
  338.5 46.1 %shard_map.309 = bf16[8,128,2048]{2,1,0:T(8,128)(2,1)} custom-call(bf16[128,2048]{1,0:T(8,128)(2,1)} %fusion.123.x_ref), custom_call_target="tpu_custom_call" | custom-call | tf_op jit(solution)/shard_map/pallas_call | solution.py:91
  384.6 7.9 %convolution_convert_fusion.4 = bf16[1024,2048]{1,0:T(8,128)(2,1)} fusion(bf16[1024,768]{1,0:T(8,128)(2,1)} %get-tuple-element.131, bf16[1024,2048]{1,0:T(8,128)(2,1)} %all-gather.7.cloned.1.call-done), kind=kOutput, calls=%fused_computation.16 | convolution fusion | flops 3223322624 | bytes 8912896 | tf_op jit(solution)/shard_map/dot_general | solution.py:490
  392.5 5.0 multiply_convert_fusion.1
  397.6 1.5 fusion.15
  400.3 1.3 fusion.30
  401.6 1.2 convolution_bitcast_fusion.4
  402.8 2.5 fusion
  405.3 1.3 fusion.2
  409.4 1.2 fusion.38
  411.6 1.9 fusion.26
  413.5 1.2 fusion.74
  414.7 1.2 multiply_reduce_fusion.12
  415.9 1.2 fusion.53
  417.2 1.4 fusion.29
  419.6 4.9 convolution_convert_fusion.5
  424.5 7.0 convolution_convert_fusion.3
  432.5 4.4 convolution_convert_fusion.7
  440.4 46.6 %shard_map.310 = f32[128,2048]{1,0:T(8,128)} custom-call(bf16[8,128,2048]{2,1,0:T(8,128)(2,1)} %bitcast.194), custom_call_target="tpu_custom_call" | custom-call | tf_op jit(solution)/shard_map/pallas_call | solution.py:161
  487.0 1.6 fusion.36
  488.7 5.7 multiply_reduce_fusion.4
  494.7 2.3 reduce-scatter.12.cloned.1.call-done
  497.0 40.9 %reduce-scatter.14.cloned.1.call-done = bf16[768,512]{1,0:T(8,128)(2,1)} async-done(((bf16[768,2048]{1,0:T(8,128)(2,1)}), bf16[768,512]{1,0:T(8,128)(2,1)}) %reduce-scatter.14.cloned.1.call-update) | async-done | bytes 786448 | tf_op jit(solution)/shard_map/reduce_scatter | solution.py:481
  537.8 5.4 multiply_reduce_fusion.2
  544.0 85.8 %reduce-scatter.6.cloned.1.call-done = bf16[128,2048]{1,0:T(8,128)(2,1)} async-done(((bf16[1024,2048]{1,0:T(8,128)(2,1)}), bf16[128,2048]{1,0:T(8,128)(2,1)}) %reduce-scatter.6.cloned.1.call-update) | async-done | bytes 524304 | tf_op jit(solution)/shard_map/reduce_scatter | solution.py:495
  629.8 3.9 fusion.39
  633.7 57.1 %reduce-scatter.10.cloned.1.call-done = bf16[512,1536]{1,0:T(8,128)(2,1)} async-done(((bf16[2048,1536]{1,0:T(8,128)(2,1)}), bf16[512,1536]{1,0:T(8,128)(2,1)}) %reduce-scatter.10.cloned.1.call-update) | async-done | bytes 1572880 | tf_op jit(solution)/shard_map/reduce_scatter | solution.py:478
  690.9 6.6 multiply_reduce_fusion
  699.2 13.7 %shard_map.311 = f32[40,128]{1,0:T(8,128)} custom-call(f32[40,128]{1,0:T(8,128)} %pad_bitcast_fusion.x_ref), custom_call_target="tpu_custom_call" | custom-call | tf_op jit(solution)/shard_map/pallas_call | solution.py:221
  713.7 1.2 fusion.54
  714.9 1.4 convolution_reduce_fusion
  716.3 1.1 convolution_reduce_fusion.1
  718.0 4.3 fusion.126
  722.4 3.0 fusion.127
  725.4 1.6 fusion.128
  (180 shorter events, 22.0 us)
Async XLA Ops:
  7.2 6.0 copy-start.3
  7.2 66.3 %all-gather.5.cloned.1.call-start = ((), (), s32[]{:S(2)}) async-start(), calls=%async_computation.5 | async-start | bytes 3932160 | tf_op jit(solution)/shard_map/all_gather | solution.py:406
  10.3 89.0 %all-gather.7.cloned.1.call-start = ((), (), s32[]{:S(2)}) async-start(), calls=%async_computation.6 | async-start | bytes 5242880 | tf_op jit(solution)/shard_map/all_gather | solution.py:408
  13.1 2.0 copy-start.40
  13.1 222.4 %all-gather.9.cloned.1.call-start = ((), (), s32[]{:S(2)}) async-start(), calls=%async_computation.7 | async-start | bytes 7864320 | tf_op jit(solution)/shard_map/all_gather | solution.py:407
  14.5 233.1 %all-gather.11.cloned.1.call-start = ((), (), s32[]{:S(2)}) async-start(), calls=%async_computation.8 | async-start | bytes 4718592 | tf_op jit(solution)/shard_map/all_gather | solution.py:468
  15.1 473.6 %reduce-scatter.8.cloned.1.call-start = ((), (), s32[]{:S(2)}) async-start(), calls=%async_computation.10 | async-start | bytes 3932160 | tf_op jit(solution)/shard_map/reduce_scatter | solution.py:556
  15.2 56.6 %copy-start.44 = (s32[1,8]{1,0:T(1,128)S(1)}, s32[1,8]{1,0:T(1,128)}, u32[]{:S(2)}) copy-start(s32[1,8]{1,0:T(1,128)} %param.42) | copy-start | bytes 100
  73.5 20.9 %copy-start.14 = (pred[512,1024]{0,1:T(8,128)(4,1)}, pred[512,1024]{0,1:T(8,128)(4,1)S(1)}, u32[]{:S(2)}) copy-start(pred[512,1024]{0,1:T(8,128)(4,1)S(1)} %fusion.18) | copy-start | bytes 1572868
  81.6 1.7 copy-start.13
  84.6 4.6 copy-start.22
  84.8 4.4 copy-start.24
  86.5 2.7 copy-start.7
  88.7 1.0 copy-start.34
  89.2 1.5 copy-start.16
  89.3 1.5 copy-start.18
  89.4 2.3 copy-start.32
  91.8 2.6 copy-start
  96.8 1.0 copy-start.28
  99.3 4.7 copy-start.30
  104.0 57.0 %copy-start.10 = (bf16[128,2048]{1,0:T(8,128)(2,1)S(1)}, bf16[128,2048]{1,0:T(8,128)(2,1)}, u32[]{:S(2)}) copy-start(bf16[128,2048]{1,0:T(8,128)(2,1)} %param.28) | copy-start | bytes 1572868
  162.5 173.6 %copy-start.5 = (f32[128,2048]{1,0:T(8,128)}, f32[128,2048]{1,0:T(8,128)S(1)}, u32[]{:S(2)}) copy-start(f32[128,2048]{1,0:T(8,128)S(1)} %get-tuple-element.128) | copy-start | bytes 3145732
  247.6 13.3 %copy-start.27 = (bf16[8,128,2048]{2,1,0:T(8,128)(2,1)S(1)}, bf16[8,128,2048]{2,1,0:T(8,128)(2,1)}, u32[]{:S(2)}) copy-start(bf16[8,128,2048]{2,1,0:T(8,128)(2,1)} %shard_map.307) | copy-start | bytes 12582916
  258.2 1.7 copy-start.48
  258.2 2.7 copy-start.49
  269.8 12.7 %copy-start.45 = (bf16[1024,2048]{1,0:T(8,128)(2,1)S(1)}, bf16[1024,2048]{1,0:T(8,128)(2,1)}, u32[]{:S(2)}) copy-start(bf16[1024,2048]{1,0:T(8,128)(2,1)} %all-gather.11.cloned.1.call-done) | copy-start | bytes 12582916
  269.8 12.7 %copy-start.46 = (bf16[1024,768]{1,0:T(8,128)(2,1)S(1)}, bf16[1024,768]{1,0:T(8,128)(2,1)}, u32[]{:S(2)}) copy-start(bf16[1024,768]{1,0:T(8,128)(2,1)} %get-tuple-element.131) | copy-start | bytes 4718596
  287.4 48.7 %copy-start.21 = (bf16[128,2048]{1,0:T(8,128)(2,1)S(1)}, bf16[128,2048]{1,0:T(8,128)(2,1)}, u32[]{:S(2)}) copy-start(bf16[128,2048]{1,0:T(8,128)(2,1)} %param.29) | copy-start | bytes 1572868
  384.6 7.9 %copy-start.29 = (f32[1024,2,128]{0,2,1:T(8,128)S(1)}, f32[1024,2,128]{0,2,1:T(8,128)}, u32[]{:S(2)}) copy-start(f32[1024,2,128]{0,2,1:T(8,128)} %copy-done.28) | copy-start | bytes 3145732
  397.6 5.2 copy-start.35
  399.1 1.2 copy-start.17
  399.1 1.2 copy-start.19
  399.7 3.1 copy-start.1
  399.7 3.1 copy-start.15
  406.6 1.0 copy-start.23
  406.6 1.2 copy-start.25
  406.6 1.8 copy-start.8
  409.3 2.3 copy-start.33
  411.6 5.5 copy-start.2
  411.6 5.5 copy-start.36
  411.6 5.5 copy-start.38
  417.1 2.2 copy-start.26
  417.1 2.3 copy-start.37
  417.2 2.4 copy-start.47
  431.5 1.0 copy-start.31
  431.5 65.5 %reduce-scatter.12.cloned.1.call-start = ((), (), s32[]{:S(2)}) async-start(), calls=%async_computation.12 | async-start | bytes 1310720 | tf_op jit(solution)/shard_map/reduce_scatter | solution.py:500
  436.9 100.9 %reduce-scatter.14.cloned.1.call-start = ((), (), s32[]{:S(2)}) async-start(), calls=%async_computation.13 | async-start | bytes 3932160 | tf_op jit(solution)/shard_map/reduce_scatter | solution.py:481
  437.7 192.1 %reduce-scatter.6.cloned.1.call-start = ((), (), s32[]{:S(2)}) async-start(), calls=%async_computation.9 | async-start | bytes 4718592 | tf_op jit(solution)/shard_map/reduce_scatter | solution.py:495
  438.4 252.4 %reduce-scatter.10.cloned.1.call-start = ((), (), s32[]{:S(2)}) async-start(), calls=%async_computation.11 | async-start | bytes 7864320 | tf_op jit(solution)/shard_map/reduce_scatter | solution.py:478
  439.2 47.8 %copy-start.11 = (bf16[128,2048]{1,0:T(8,128)(2,1)S(1)}, bf16[128,2048]{1,0:T(8,128)(2,1)}, u32[]{:S(2)}) copy-start(bf16[128,2048]{1,0:T(8,128)(2,1)} %param.28) | copy-start | bytes 1572868
  488.7 49.1 %copy-start.6 = (f32[1024,512]{1,0:T(8,128)S(1)}, f32[1024,512]{1,0:T(8,128)}, u32[]{:S(2)}) copy-start(f32[1024,512]{1,0:T(8,128)} %param.32) | copy-start | bytes 6291460
  544.0 146.9 %copy-start.4 = (f32[512,1536]{1,0:T(8,128)S(1)}, f32[512,1536]{1,0:T(8,128)}, u32[]{:S(2)}) copy-start(f32[512,1536]{1,0:T(8,128)} %param.31) | copy-start | bytes 9437188
  718.0 4.3 copy-start.12
  722.4 3.0 copy-start.9
  722.4 3.0 copy-start.20
  725.3 1.7 copy-start.39
  725.4 1.7 copy-start.41
  725.4 1.7 copy-start.42
  725.4 1.7 copy-start.43
Sparse Core Ops, SparseCore 0:
  10.4 31.2 all-gather.4
  43.8 34.4 all-gather.6
  80.5 46.3 all-gather.8
  128.8 105.6 all-gather.10
  431.6 37.5 reduce-scatter.7
  472.2 24.7 reduce-scatter.11
  500.1 37.7 reduce-scatter.13
  541.5 88.2 reduce-scatter.5
  632.3 58.4 reduce-scatter.9

commit v3 on v2

--- a/solution.py
+++ b/solution.py
@@ -7,6 +7,7 @@
 from jax.experimental import pallas as pl
 from jax.experimental.pallas import tpu as pltpu
 from jax.sharding import PartitionSpec as P
+
 
 norm_epsilon = 1e-06
 rope_base = 1000000.0
@@ -22,6 +23,7 @@
 
 def remote(src, dst, ssem, rsem, dev):
     return pltpu.make_async_remote_copy(src_ref=src, dst_ref=dst, send_sem=ssem, recv_sem=rsem, device_id=dev, device_id_type=MESH)
+
 
 def enter(Z, z, y):
     bar = pltpu.get_barrier_semaphore()
@@ -37,6 +39,7 @@
     def _(): pl.semaphore_wait(bar, 3)
     @pl.when(jnp.logical_not(inner))
     def _(): pl.semaphore_wait(bar, 2)
+
 
 def ag_kernel(Z, C, x_ref, out_ref, usem, dsem, ysem, rsem):
     z = lax.axis_index("mlp"); y = lax.axis_index("head")
@@ -86,17 +89,20 @@
             @pl.when((z > 0) & (zb >= z))
             def _(): dn(blk(b, c), b, zb, c).wait_send()
 
+
 def ag(x, Z, C, cid=1):
     R, D = x.shape
     return pl.pallas_call(functools.partial(ag_kernel, Z, C),
         out_shape=jax.ShapeDtypeStruct((2 * Z, R, D), x.dtype),
         in_specs=[pl.BlockSpec(memory_space=pltpu.VMEM)], out_specs=pl.BlockSpec(memory_space=pltpu.VMEM),
         scratch_shapes=[pltpu.SemaphoreType.DMA((Z, C))] * 3 + [pltpu.SemaphoreType.DMA((2 * Z, C))],
+        cost_estimate=pl.CostEstimate(flops=0, bytes_accessed=160_000_000, transcendentals=0),
         compiler_params=pltpu.CompilerParams(collective_id=cid, has_side_effects=True, vmem_limit_bytes=60 << 20))(x)
+
 
 def rs_kernel(Z, C, p_ref, out_ref, ybuf, bbuf, abuf, ubuf, dbuf, ysem, usem, dsem, yr, br, ar):
     z = lax.axis_index("mlp"); y = lax.axis_index("head")
-    R, D = out_ref.shape; r = R // C
+    R, _ = out_ref.shape; r = R // C
     enter(Z, z, y)
     def rows(c): return pl.ds(c * r, r)
     def yy(zb, c): return remote(p_ref.at[zb * 2 + 1 - y, rows(c)], ybuf.at[zb, rows(c)], ysem.at[zb, c], yr.at[zb, c], {"head": 1 - y})
@@ -156,12 +162,14 @@
             @pl.when(zb < z)
             def _(): dn(zb, c).wait_send()
 
+
 def rs(p, Z, C, cid=2):
     _, R, D = p.shape
     return pl.pallas_call(functools.partial(rs_kernel, Z, C),
         out_shape=jax.ShapeDtypeStruct((R, D), jnp.float32),
         in_specs=[pl.BlockSpec(memory_space=pltpu.VMEM)], out_specs=pl.BlockSpec(memory_space=pltpu.VMEM),
         scratch_shapes=[pltpu.VMEM((Z, R, D), p.dtype)] * 5 + [pltpu.SemaphoreType.DMA((Z, C))] * 6,
+        cost_estimate=pl.CostEstimate(flops=0, bytes_accessed=160_000_000, transcendentals=0),
         compiler_params=pltpu.CompilerParams(collective_id=cid, has_side_effects=True, vmem_limit_bytes=60 << 20))(p)
 
 
@@ -238,6 +246,11 @@
 def scatter_rows(partial, cid):
     levels = lax.axis_size("mlp")
     return rs(partial.reshape(2 * levels, -1, partial.shape[1]), levels, 2, cid)
+
+
+def scatter_seq(gradient, dimension):
+    part = lax.psum_scatter(gradient, "seq", scatter_dimension=dimension, tiled=True)
+    return part.astype(jnp.float32)
 
 
 def scaled_norm(values, norm_gain):
@@ -475,12 +488,8 @@
             contract_last(delta_gate_up, forward_reduced).astype(jnp.bfloat16),
         )
     )
-    feed_total = lax.psum_scatter(
-        feed_gradient, "seq", scatter_dimension=0, tiled=True
-    ).astype(jnp.float32)
-    down_total = lax.psum_scatter(
-        down_gradient, "seq", scatter_dimension=1, tiled=True
-    ).astype(jnp.float32)
+    feed_total = scatter_seq(feed_gradient, 0)
+    down_total = scatter_seq(down_gradient, 1)
     delta_normed_two = scatter_rows(feed_delta_partial, 4)
     delta_middle_part, delta_gain_two = back_two(delta_normed_two)
     delta_middle = cotangent.astype(jnp.float32) + delta_middle_part
@@ -497,12 +506,7 @@
     ).astype(jnp.float32)
     block_output = (middle + feed_out).astype(jnp.bfloat16)
     delta_gated = contract_last(branch_rows, mixer_low)
-    mixer_total = lax.psum_scatter(
-        contract_first(gated_low, branch_rows).astype(jnp.bfloat16),
-        "seq",
-        scatter_dimension=1,
-        tiled=True,
-    ).astype(jnp.float32)
+    mixer_total = scatter_seq(contract_first(gated_low, branch_rows).astype(jnp.bfloat16), 1)
     delta_attended = delta_gated * gate_sigmoid
     delta_logits = delta_gated * attended_rows * gate_sigmoid * (1.0 - gate_sigmoid)
     delta_attended_low = delta_attended.astype(jnp.bfloat16).reshape(
@@ -553,9 +557,7 @@
             contract_last(delta_projected, attention_reduced).astype(jnp.bfloat16),
         )
     )
-    attention_total = lax.psum_scatter(
-        attention_gradient, "seq", scatter_dimension=0, tiled=True
-    ).astype(jnp.float32)
+    attention_total = scatter_seq(attention_gradient, 0)
     delta_normed = scatter_rows(delta_partial, 6)
     delta_input_part, delta_gain_one = back_one(delta_normed)
     input_gradient = delta_middle + delta_input_part
@@ -673,6 +675,7 @@
         P("seq", None),
         P(),
     )
+
     return jax.shard_map(
         shards,
         mesh=mesh,

time: 741 us -> 741 us (level)
  no operation moved by 1% of the time
where the time goes in v3:
time: 741 us; the launch traced here: 735 us
  Pallas kernels  336 us (45%)
  waiting for transfers between devices  189 us (26%)
  matrix products  114 us (15%)
  other arithmetic  67.3 us (9%)
  between operations  16 us (2%)
  local copies, waits for them, and re-layouts  12.3 us (2%)
    pallas_call x3, Pallas kernels, ag(): pl.pallas_call(functools.partial(ag_kernel, Z, C), out_shape=jax.ShapeDty...  171 us
    pallas_call x3, Pallas kernels, rs(): pl.pallas_call(functools.partial(rs_kernel, Z, C), out_shape=jax.ShapeDty...  151 us
    reduce_scatter x4, waiting for transfers between devices, scatter_seq(): lax.psum_scatter(gradient, 'seq', scatter_dimension=dimension, tiled=True)  100 us
    reduce_scatter x1, waiting for transfers between devices, shards(): lax.psum_scatter(feed_out_partial, ('mlp', 'head'), scatter_dimension=0,...  85.8 us
    dot_general x4, matrix products, contract_last(): lax.dot_general(left, right, (((1,), (1,)), ((), ())), preferred_element_...  35.3 us
    dot_general x4, matrix products, contract_first(): lax.dot_general(left, right, (((0,), (0,)), ((), ())), preferred_element_...  23.1 us
    reduce_sum x4, other arithmetic, kind_sums(): jnp.sum(matrix * matrix, axis=over_axis)  20.7 us
  transfers between devices with their start and end apart: 9, of which 4 were waited for; matrix products, arithmetic and copies ran while one was open for 10% of the time, Pallas kernels for 31%

profile of v3, /device:TPU:0, one launch (start us, length us, event | category | flops | bytes accessed | tf_op | source)
XLA Modules:
  0.0 734.6 jit_solution(4755075249460581432)
XLA Ops:
  7.2 3.1 multiply_reduce_fusion.5
  10.4 2.7 convert_element_type.150
  13.2 1.3 convert_element_type.154
  15.2 1.2 fusion.40
  16.5 2.0 fusion.35.x_ref
  18.5 53.3 %shard_map.305 = bf16[8,128,2048]{2,1,0:T(8,128)(2,1)} custom-call(bf16[128,2048]{1,0:T(8,128)(2,1)} %fusion.35.x_ref), custom_call_target="tpu_custom_call" | custom-call | bytes 160000000 | tf_op jit(solution)/shard_map/pallas_call | solution.py:95
  73.5 8.1 %fusion.139 = (bf16[1024,768]{0,1:T(8,128)(2,1)}, f32[1024,768]{0,1:T(8,128)S(1)}) fusion(bf16[1024,2048]{1,0:T(8,128)(2,1)} %bitcast.196, bf16[2048,768]{1,0:T(8,128)(2,1)} %all-gather.5.cloned.1.call-done), kind=kOutput, calls=%fused_computation.261 | convolution fusion | flops 3222011904 | bytes 12058624 | tf_op jit(solution)/shard_map/dot_general | solution.py:430
  81.8 1.4 fusion.71
  83.3 1.1 slice.202
  84.8 1.7 copy.58
  86.6 1.8 multiply_reduce_fusion.11
  90.7 1.0 fusion.12
  92.8 1.5 convolution_bitcast_fusion.3
  94.4 2.3 convolution_bitcast_fusion.2
  97.8 1.6 fusion.45
  99.4 4.6 convolution_convert_fusion.2
  104.0 57.0 %shard_map.306 = f32[128,2048]{1,0:T(8,128)} custom-call(bf16[8,128,2048]{2,1,0:T(8,128)(2,1)} %bitcast.193), custom_call_target="tpu_custom_call" | custom-call | bytes 160000000 | tf_op jit(solution)/shard_map/pallas_call | solution.py:168
  161.0 1.4 multiply_reduce_fusion.10
  162.5 1.1 multiply_convert_fusion.2.x_ref
  163.6 71.9 %shard_map.307 = bf16[8,128,2048]{2,1,0:T(8,128)(2,1)} custom-call(bf16[128,2048]{1,0:T(8,128)(2,1)} %multiply_convert_fusion.2.x_ref), custom_call_target="tpu_custom_call" | custom-call | bytes 160000000 | tf_op jit(solution)/shard_map/pallas_call | solution.py:95
  235.5 12.1 %fusion.141 = f32[1024,1536]{1,0:T(8,128)} fusion(bf16[1024,2048]{1,0:T(8,128)(2,1)} %bitcast.200, bf16[2048,1536]{1,0:T(8,128)(2,1)} %all-gather.9.cloned.1.call-done), kind=kOutput, calls=%fused_computation.263 | convolution fusion | flops 6442450944 | bytes 16777216 | tf_op jit(solution)/shard_map/dot_general | solution.py:478
  247.6 10.6 %fusion.66 = (f32[1024,768]{1,0:T(8,128)S(1)}, f32[1024,768]{1,0:T(8,128)S(1)}, bf16[1024,768]{1,0:T(8,128)(2,1)}) fusion(f32[1024,1536]{1,0:T(8,128)} %fusion.141, bf16[1024,2048]{1,0:T(8,128)(2,1)} %all-gather.11.cloned.1.call-done, bf16[1024,2048]{1,0:T(8,128)(2,1)} %all-gather.7.cloned.1.call-done), kind=kOutput, calls=%fused_computation.168 | convolution fusion | flops 3232235520 | bytes 21495808 | tf_op jit(solution)/shard_map/dot_general | solution.py:352
  258.2 1.7 copy-done.48
  259.8 1.0 copy-done.49
  260.9 8.9 %convolution_convert_fusion = bf16[2048,1536]{1,0:T(8,128)(2,1)} fusion(bf16[1024,2048]{1,0:T(8,128)(2,1)S(1)} %bitcast.201, f32[1024,768]{1,0:T(8,128)S(1)} %get-tuple-element.130, f32[1024,768]{1,0:T(8,128)S(1)} %get-tuple-element.129), kind=kOutput, calls=%fused_computation | convolution fusion | flops 6448742400 | bytes 16777216 | tf_op jit(solution)/shard_map/dot_general | solution.py:346
  269.8 12.7 %convolution_convert_fusion.1 = bf16[1024,2048]{1,0:T(8,128)(2,1)} fusion(bf16[2048,1536]{1,0:T(8,128)(2,1)} %all-gather.9.cloned.1.call-done, f32[1024,768]{1,0:T(8,128)} %copy-done.49, f32[1024,768]{1,0:T(8,128)} %copy-done.48), kind=kOutput, calls=%fused_computation.13 | convolution fusion | flops 6447693824 | bytes 16777216 | tf_op jit(solution)/shard_map/dot_general | solution.py:352
  282.5 4.8 convolution_convert_fusion.6
  287.4 47.2 %shard_map.308 = f32[128,2048]{1,0:T(8,128)} custom-call(bf16[8,128,2048]{2,1,0:T(8,128)(2,1)} %bitcast.195), custom_call_target="tpu_custom_call" | custom-call | bytes 160000000 | tf_op jit(solution)/shard_map/pallas_call | solution.py:168
  334.6 1.5 multiply_reduce_fusion.7
  336.1 2.4 fusion.123.x_ref
  338.5 46.1 %shard_map.309 = bf16[8,128,2048]{2,1,0:T(8,128)(2,1)} custom-call(bf16[128,2048]{1,0:T(8,128)(2,1)} %fusion.123.x_ref), custom_call_target="tpu_custom_call" | custom-call | bytes 160000000 | tf_op jit(solution)/shard_map/pallas_call | solution.py:95
  384.6 7.9 %convolution_convert_fusion.4 = bf16[1024,2048]{1,0:T(8,128)(2,1)} fusion(bf16[1024,768]{1,0:T(8,128)(2,1)} %get-tuple-element.131, bf16[1024,2048]{1,0:T(8,128)(2,1)} %all-gather.7.cloned.1.call-done), kind=kOutput, calls=%fused_computation.16 | convolution fusion | flops 3223322624 | bytes 8912896 | tf_op jit(solution)/shard_map/dot_general | solution.py:499
  392.5 5.0 multiply_convert_fusion.1
  397.6 1.5 fusion.15
  400.3 1.3 fusion.30
  401.6 1.2 convolution_bitcast_fusion.4
  402.8 2.5 fusion
  405.3 1.3 fusion.2
  409.4 1.2 fusion.38
  411.6 1.9 fusion.26
  413.5 1.2 fusion.74
  414.7 1.2 multiply_reduce_fusion.12
  415.9 1.2 fusion.53
  417.2 1.4 fusion.29
  419.6 4.9 convolution_convert_fusion.5
  424.5 7.0 convolution_convert_fusion.3
  432.5 4.4 convolution_convert_fusion.7
  440.4 46.6 %shard_map.310 = f32[128,2048]{1,0:T(8,128)} custom-call(bf16[8,128,2048]{2,1,0:T(8,128)(2,1)} %bitcast.194), custom_call_target="tpu_custom_call" | custom-call | bytes 160000000 | tf_op jit(solution)/shard_map/pallas_call | solution.py:168
  487.0 1.6 fusion.36
  488.7 5.7 multiply_reduce_fusion.4
  494.7 2.3 reduce-scatter.12.cloned.1.call-done
  497.0 40.9 %reduce-scatter.14.cloned.1.call-done = bf16[768,512]{1,0:T(8,128)(2,1)} async-done(((bf16[768,2048]{1,0:T(8,128)(2,1)}), bf16[768,512]{1,0:T(8,128)(2,1)}) %reduce-scatter.14.cloned.1.call-update) | async-done | bytes 786448 | tf_op jit(solution)/shard_map/reduce_scatter | solution.py:252
  537.8 5.4 multiply_reduce_fusion.2
  544.0 85.8 %reduce-scatter.6.cloned.1.call-done = bf16[128,2048]{1,0:T(8,128)(2,1)} async-done(((bf16[1024,2048]{1,0:T(8,128)(2,1)}), bf16[128,2048]{1,0:T(8,128)(2,1)}) %reduce-scatter.6.cloned.1.call-update) | async-done | bytes 524304 | tf_op jit(solution)/shard_map/reduce_scatter | solution.py:504
  629.8 3.9 fusion.39
  633.7 57.1 %reduce-scatter.10.cloned.1.call-done = bf16[512,1536]{1,0:T(8,128)(2,1)} async-done(((bf16[2048,1536]{1,0:T(8,128)(2,1)}), bf16[512,1536]{1,0:T(8,128)(2,1)}) %reduce-scatter.10.cloned.1.call-update) | async-done | bytes 1572880 | tf_op jit(solution)/shard_map/reduce_scatter | solution.py:252
  690.9 6.6 multiply_reduce_fusion
  699.2 13.7 %shard_map.311 = f32[40,128]{1,0:T(8,128)} custom-call(f32[40,128]{1,0:T(8,128)} %pad_bitcast_fusion.x_ref), custom_call_target="tpu_custom_call" | custom-call | tf_op jit(solution)/shard_map/pallas_call | solution.py:229
  713.7 1.2 fusion.54
  714.9 1.4 convolution_reduce_fusion
  716.3 1.1 convolution_reduce_fusion.1
  718.0 4.3 fusion.126
  722.4 3.0 fusion.127
  725.4 1.6 fusion.128
  (180 shorter events, 22.0 us)
Async XLA Ops:
  7.2 6.0 copy-start.3
  7.2 66.3 %all-gather.5.cloned.1.call-start = ((), (), s32[]{:S(2)}) async-start(), calls=%async_computation.5 | async-start | bytes 3932160 | tf_op jit(solution)/shard_map/all_gather | solution.py:419
  10.3 89.0 %all-gather.7.cloned.1.call-start = ((), (), s32[]{:S(2)}) async-start(), calls=%async_computation.6 | async-start | bytes 5242880 | tf_op jit(solution)/shard_map/all_gather | solution.py:421
  13.1 2.0 copy-start.40
  13.1 222.4 %all-gather.9.cloned.1.call-start = ((), (), s32[]{:S(2)}) async-start(), calls=%async_computation.7 | async-start | bytes 7864320 | tf_op jit(solution)/shard_map/all_gather | solution.py:420
  14.5 233.1 %all-gather.11.cloned.1.call-start = ((), (), s32[]{:S(2)}) async-start(), calls=%async_computation.8 | async-start | bytes 4718592 | tf_op jit(solution)/shard_map/all_gather | solution.py:481
  15.1 473.6 %reduce-scatter.8.cloned.1.call-start = ((), (), s32[]{:S(2)}) async-start(), calls=%async_computation.10 | async-start | bytes 3932160 | tf_op jit(solution)/shard_map/reduce_scatter | solution.py:252
  15.2 56.6 %copy-start.44 = (s32[1,8]{1,0:T(1,128)S(1)}, s32[1,8]{1,0:T(1,128)}, u32[]{:S(2)}) copy-start(s32[1,8]{1,0:T(1,128)} %param.42) | copy-start | bytes 100
  73.5 20.9 %copy-start.14 = (pred[512,1024]{0,1:T(8,128)(4,1)}, pred[512,1024]{0,1:T(8,128)(4,1)S(1)}, u32[]{:S(2)}) copy-start(pred[512,1024]{0,1:T(8,128)(4,1)S(1)} %fusion.18) | copy-start | bytes 1572868
  81.6 1.7 copy-start.13
  84.6 4.6 copy-start.22
  84.8 4.4 copy-start.24
  86.5 2.7 copy-start.7
  88.7 1.0 copy-start.34
  89.2 1.5 copy-start.16
  89.3 1.5 copy-start.18
  89.4 2.3 copy-start.32
  91.8 2.6 copy-start
  96.8 1.0 copy-start.28
  99.3 4.7 copy-start.30
  104.0 57.0 %copy-start.10 = (bf16[128,2048]{1,0:T(8,128)(2,1)S(1)}, bf16[128,2048]{1,0:T(8,128)(2,1)}, u32[]{:S(2)}) copy-start(bf16[128,2048]{1,0:T(8,128)(2,1)} %param.28) | copy-start | bytes 1572868
  162.5 173.6 %copy-start.5 = (f32[128,2048]{1,0:T(8,128)}, f32[128,2048]{1,0:T(8,128)S(1)}, u32[]{:S(2)}) copy-start(f32[128,2048]{1,0:T(8,128)S(1)} %get-tuple-element.128) | copy-start | bytes 3145732
  247.6 13.3 %copy-start.27 = (bf16[8,128,2048]{2,1,0:T(8,128)(2,1)S(1)}, bf16[8,128,2048]{2,1,0:T(8,128)(2,1)}, u32[]{:S(2)}) copy-start(bf16[8,128,2048]{2,1,0:T(8,128)(2,1)} %shard_map.307) | copy-start | bytes 12582916
  258.2 1.7 copy-start.48
  258.2 2.7 copy-start.49
  269.8 12.7 %copy-start.45 = (bf16[1024,2048]{1,0:T(8,128)(2,1)S(1)}, bf16[1024,2048]{1,0:T(8,128)(2,1)}, u32[]{:S(2)}) copy-start(bf16[1024,2048]{1,0:T(8,128)(2,1)} %all-gather.11.cloned.1.call-done) | copy-start | bytes 12582916
  269.8 12.7 %copy-start.46 = (bf16[1024,768]{1,0:T(8,128)(2,1)S(1)}, bf16[1024,768]{1,0:T(8,128)(2,1)}, u32[]{:S(2)}) copy-start(bf16[1024,768]{1,0:T(8,128)(2,1)} %get-tuple-element.131) | copy-start | bytes 4718596
  287.4 48.7 %copy-start.21 = (bf16[128,2048]{1,0:T(8,128)(2,1)S(1)}, bf16[128,2048]{1,0:T(8,128)(2,1)}, u32[]{:S(2)}) copy-start(bf16[128,2048]{1,0:T(8,128)(2,1)} %param.29) | copy-start | bytes 1572868
  384.6 7.9 %copy-start.29 = (f32[1024,2,128]{0,2,1:T(8,128)S(1)}, f32[1024,2,128]{0,2,1:T(8,128)}, u32[]{:S(2)}) copy-start(f32[1024,2,128]{0,2,1:T(8,128)} %copy-done.28) | copy-start | bytes 3145732
  397.6 5.2 copy-start.35
  399.1 1.2 copy-start.17
  399.1 1.2 copy-start.19
  399.7 3.1 copy-start.1
  399.7 3.1 copy-start.15
  406.6 1.0 copy-start.23
  406.6 1.2 copy-start.25
  406.6 1.8 copy-start.8
  409.3 2.3 copy-start.33
  411.6 5.5 copy-start.2
  411.6 5.5 copy-start.36
  411.6 5.5 copy-start.38
  417.1 2.2 copy-start.26
  417.1 2.3 copy-start.37
  417.2 2.4 copy-start.47
  431.5 1.0 copy-start.31
  431.5 65.5 %reduce-scatter.12.cloned.1.call-start = ((), (), s32[]{:S(2)}) async-start(), calls=%async_computation.12 | async-start | bytes 1310720 | tf_op jit(solution)/shard_map/reduce_scatter | solution.py:252
  436.9 100.9 %reduce-scatter.14.cloned.1.call-start = ((), (), s32[]{:S(2)}) async-start(), calls=%async_computation.13 | async-start | bytes 3932160 | tf_op jit(solution)/shard_map/reduce_scatter | solution.py:252
  437.7 192.1 %reduce-scatter.6.cloned.1.call-start = ((), (), s32[]{:S(2)}) async-start(), calls=%async_computation.9 | async-start | bytes 4718592 | tf_op jit(solution)/shard_map/reduce_scatter | solution.py:504
  438.4 252.4 %reduce-scatter.10.cloned.1.call-start = ((), (), s32[]{:S(2)}) async-start(), calls=%async_computation.11 | async-start | bytes 7864320 | tf_op jit(solution)/shard_map/reduce_scatter | solution.py:252
  439.2 47.8 %copy-start.11 = (bf16[128,2048]{1,0:T(8,128)(2,1)S(1)}, bf16[128,2048]{1,0:T(8,128)(2,1)}, u32[]{:S(2)}) copy-start(bf16[128,2048]{1,0:T(8,128)(2,1)} %param.28) | copy-start | bytes 1572868
  488.7 49.1 %copy-start.6 = (f32[1024,512]{1,0:T(8,128)S(1)}, f32[1024,512]{1,0:T(8,128)}, u32[]{:S(2)}) copy-start(f32[1024,512]{1,0:T(8,128)} %param.32) | copy-start | bytes 6291460
  544.0 146.9 %copy-start.4 = (f32[512,1536]{1,0:T(8,128)S(1)}, f32[512,1536]{1,0:T(8,128)}, u32[]{:S(2)}) copy-start(f32[512,1536]{1,0:T(8,128)} %param.31) | copy-start | bytes 9437188
  718.0 4.3 copy-start.12
  722.4 3.0 copy-start.9
  722.4 3.0 copy-start.20
  725.3 1.7 copy-start.39
  725.4 1.7 copy-start.41
  725.4 1.7 copy-start.42
  725.4 1.7 copy-start.43
Sparse Core Ops, SparseCore 0:
  10.4 31.2 all-gather.4
  43.8 34.4 all-gather.6
  80.5 46.3 all-gather.8
  128.8 105.6 all-gather.10
  431.6 37.5 reduce-scatter.7
  472.2 24.7 reduce-scatter.11
  500.1 37.7 reduce-scatter.13
  541.5 88.2 reduce-scatter.5
  632.3 58.4 reduce-scatter.9
